TPU v7x, 32 devices: a whole 2x2x4 slice. The times are simulated.
32 devices in a mesh: shard: 4 (over x, core), rep: 8 (over z, y).
Axes of the slice: x: 2, y: 2, z: 4, core: 2. Of those that a mesh axis runs over, the one named last changes fastest.
Arguments:
- tokens: bfloat16 [12288, 4608], P(('shard', 'rep')), may hold values from -6 to 6
- norm_gain: float32 [4608], replicated, may hold values from 0.25 to 1.75
- key_grad: bfloat16 [12288, 1024], P(('shard', 'rep')), may hold values from -6 to 6
- key_weight: bfloat16 [4608, 1024], P('shard'), may hold values from -0.09375 to 0.09375
- m_code: bfloat16 [4608, 1024], P('shard'), may hold values from -127 to 127, as said below
- m_exp: int32 [4608, 4], P('shard'), may hold values from 3 to 7
- v_code: bfloat16 [4608, 1024], P('shard'), may hold values from 1 to 255, as said below
- v_exp: int32 [4608, 4], P('shard'), may hold values from 4 to 9
Outputs:
- keys: bfloat16 [12288, 1024], P(('shard', 'rep'))
- token_grad: bfloat16 [12288, 4608], P(('shard', 'rep'))
- adam_step: float32 [4608, 1024], P('shard')
- m_rel: bfloat16 [4608, 1024], P('shard')
- m_scale: float32 [4608, 4], P('shard')
- v_rel: bfloat16 [4608, 1024], P('shard')
- v_scale: float32 [4608, 4], P('shard')
Inputs may be any that keep to these rules, and one draw needn't show every extreme that they name: `m_code`: whole numbers. `v_code`: whole numbers.
All inputs are finite; a program needn't handle non-finite values. Where the computation divides by a largest or mean magnitude, that divisor is 1e-20 or more.
Results may differ from a plain program's by a relative error of at most 0.0099.
Values may be sent and summed in bfloat16 or wider, within the bound.
A program may use at most 192 MiB of HBM per device.

v0:
```python
import functools

import jax
import jax.numpy as jnp
from jax import lax
from jax.experimental import pallas as pl
from jax.experimental.pallas import tpu as pltpu
from jax.sharding import PartitionSpec as P

bias_first = 0.9999734386011124
bias_second = 0.0952078528862904
F32 = jnp.float32
BF16 = jnp.bfloat16

HALVES = [("x", "y", "l"), ("y", "l", "x"), ("l", "x", "y"), ("x", "y", "l")]
DOUBLES = [("l", "y"), ("y", "l"), ("l", "y"), ("y", "l")]
HELPERS = ["y", "l", "y", "l"]
ORDER = [
    "WX0", "WX1", "NORM", "T0", "T1", "O0", "T2", "O1", "T3", "WF0", "WF1", "WC", "O2", "O3",
    "C20", "C21", "WG0", "WG1", "C22", "MO", "C30", "C31", "C23", "C32", "MC", "WX2", "WX3",
    "C40", "C41", "C42", "C33", "C50", "C51", "C52", "C43", "C60", "C61", "C62", "WF2", "WF3", "C53",
    "C70", "C71", "C72", "WG2", "WG3", "MF", "C63", "MG", "FIN", "C73",
]


def bits_of(count):
    bits = count.bit_length() - 1
    assert 1 << bits == count
    return bits


class Labels:
    def __init__(self, counts):
        shards, reps = bits_of(counts["shard"]), bits_of(counts["rep"])
        assert shards == 2 and reps >= 2
        self.me = {axis: lax.axis_index(axis) for axis in ("shard", "rep")}
        self.of = {"c": ("shard", 0), "x": ("shard", 1), "y": ("rep", 0), "l": ("rep", 1)}
        self.extra = [f"h{n}" for n in range(2, reps)]
        for n in range(2, reps):
            self.of[f"h{n}"] = ("rep", n)
        self.bit = {}
        for label, (axis, n) in self.of.items():
            self.bit[label] = lax.rem(lax.div(self.me[axis], jnp.int32(1 << n)), jnp.int32(2))

    def device(self, label):
        axis, n = self.of[label]
        return {axis: self.me[axis] + (1 << n) - 2 * (1 << n) * self.bit[label]}


def tiled(rows, step, body):
    def run(i, carry):
        body(pl.ds(pl.multiple_of(i * step, step), step))
        return carry

    lax.fori_loop(0, rows // step, run, 0)


def step_of(rows, most):
    for step in range(most, 0, -1):
        if rows % step == 0 and step % 16 == 0:
            return step
    return rows


def layer_kernel(counts, tokens, gain, key_grad, weight, keys, token_grad, grads, *scratch):
    (x, gains, kg, normed, turned, full, own, th, kc, s1, r1, s2, r2, s3, r3, hs, hr, got, kacc, dn, tg, kout, invs,
     load_sem, out_sem, core_sem, one_sem, two_sem, three_sem, h_sem, a_sem, w_sem, wc_sem, wo_sem) = scratch
    lab = Labels(counts)
    bit = lab.bit
    tokens_here, features = x.shape
    groups, _, _, part, wide = own.shape
    rows = 4 * part
    width = kg.shape[1]
    shard = lab.me["shard"]
    core = bit["c"]
    unit = rows // (2 * len(HELPERS))

    def local(src, dst, sem):
        return pltpu.make_async_copy(src, dst, sem)

    def remote(src, dst, sems, label):
        return pltpu.make_async_remote_copy(
            src_ref=src, dst_ref=dst, send_sem=sems.at[0], recv_sem=sems.at[1],
            device_id=lab.device(label), device_id_type=pl.DeviceIdType.MESH,
        )

    sent = []

    def send(copy):
        copy.start()
        sent.append(copy)
        return copy

    third = tokens_here // 3
    loads = [local(tokens.at[pl.ds(n * third, third)], x.at[pl.ds(n * third, third)], load_sem.at[n]) for n in range(3)]
    load_gain = local(gain, gains, load_sem.at[3])
    load_kg = local(key_grad, kg, load_sem.at[4])
    load_w = local(weight, full.at[shard], load_sem.at[5])
    load_gain.start()
    for load in loads:
        load.start()
    load_kg.start()
    load_w.start()

    barrier = pltpu.get_barrier_semaphore()
    for label in lab.of:
        pl.semaphore_signal(barrier, inc=1, device_id=lab.device(label), device_id_type=pl.DeviceIdType.MESH)
    pl.semaphore_wait(barrier, len(lab.of))

    far = shard + 2 - 4 * bit["x"]
    near = shard + 1 - 2 * core
    both = far + 1 - 2 * core

    def rows_at(place):
        return (2 * place["x"] + place["c"]) * rows + (2 * place["y"] + place["l"]) * part

    tasks = {}

    def unit_at(n, side):
        return pl.ds(pl.multiple_of((2 * n + side) * unit, 16 if unit % 16 == 0 else unit), unit)

    def weight_copies(n):
        side = bit[HELPERS[n]]
        mine, other = unit_at(n, side), unit_at(n, 1 - side)
        return dict(
            wx=remote(weight.at[mine], full.at[shard, mine], w_sem.at[n, 0], "x"),
            wf=remote(full.at[far, mine], full.at[far, mine], w_sem.at[n, 1], HELPERS[n]),
            wc=remote(full.at[far, mine], full.at[far, mine], wc_sem.at[n, 0], "c"),
            wd=remote(full.at[far, other], full.at[far, other], wc_sem.at[n, 1], "c"),
        )

    parts = [weight_copies(n) for n in range(len(HELPERS))]

    def weight_task(n):
        def wx():
            send(parts[n]["wx"])

        def wf():
            parts[n]["wx"].wait_recv()
            send(parts[n]["wf"])
            send(parts[n]["wc"])

        def wg():
            parts[n]["wf"].wait_recv()
            send(parts[n]["wd"])

        tasks[f"WX{n}"], tasks[f"WF{n}"], tasks[f"WG{n}"] = wx, wf, wg

    for n in range(len(HELPERS)):
        weight_task(n)
    own_copy = remote(full.at[shard], full.at[shard], wo_sem, "c")

    def weight_core():
        load_w.wait()
        send(own_copy)

    tasks["WC"] = weight_core

    def norm():
        load_gain.wait()
        flat = jnp.concatenate([gains[k : k + 1, :] for k in range(features // gains.shape[1])], axis=1)

        def block(at):
            value = x[at, :].astype(F32)
            inv = lax.rsqrt(jnp.mean(value * value, axis=1, keepdims=True) + 1e-06)
            invs[at, :] = inv
            normed[at, :] = (value * inv * flat).astype(BF16)

        for n in range(3):
            loads[n].wait()

            def run(i, carry):
                block(pl.ds(pl.multiple_of(n * third + i * 16, 16), 16))
                return carry

            lax.fori_loop(0, third // 16, run, 0)

        def turn(at):
            turned[at, :] = normed[:, at].T

        tiled(features, 128, turn)
        load_kg.wait()

    tasks["NORM"] = norm

    def outer(place, g):
        at = pl.ds(pl.multiple_of(rows_at(place), 16), part)
        return jnp.dot(turned[at, :], kg[:, g * wide : (g + 1) * wide], preferred_element_type=F32)

    core_copies = [remote(th.at[g], kc.at[g], core_sem.at[g], "c") for g in range(groups)]

    def group_tasks(g):
        o1, o2, o3 = HALVES[g]
        a1, a2 = DOUBLES[g]
        b1, b2, b3 = bit[o1], bit[o2], bit[o3]

        def theirs():
            def run(t, carry):
                a, b = t // 4, t % 4
                place = {"x": a, "c": 1 - core, "y": b // 2, "l": b % 2}
                th[g, a, b] = outer(place, g).astype(BF16)
                return carry

            lax.fori_loop(0, 8, run, 0)
            send(core_copies[g])

        one = [remote(s1.at[g, j], r1.at[g, j], one_sem.at[g, n], o1) for n, j in enumerate((1 - b2, b2))]
        two = [remote(s2.at[g, j], r2.at[g, j], two_sem.at[g, n], o2) for n, j in enumerate((1 - b3, b3))]
        three = remote(s3.at[g], r3.at[g], three_sem.at[g], o3)
        more = [remote(hs.at[g, n], hr.at[g, n], h_sem.at[g, n], label) for n, label in enumerate(lab.extra)]
        spot = {"y": bit["y"], "l": bit["l"]}
        mine = got.at[g, spot["y"], spot["l"]]
        across = dict(spot)
        across[a1] = 1 - spot[a1]
        other = got.at[g, across["y"], across["l"]]
        up1 = remote(mine, mine, a_sem.at[g, 0], a1)
        up2 = remote(mine, mine, a_sem.at[g, 1], a2)
        up3 = remote(other, other, a_sem.at[g, 2], a2)

        def ours():
            core_copies[g].wait_recv()

            def piece(first, second, third_bit):
                place = {o1: first, o2: second, o3: third_bit, "c": core}
                came = kc[g, place["x"], 2 * place["y"] + place["l"]]
                return outer(place, g) + came.astype(F32)

            for n, j in enumerate((1 - b2, b2)):
                def run(t, carry):
                    s1[g, j, t] = piece(1 - b1, j, t).astype(BF16)
                    return carry

                lax.fori_loop(0, 2, run, 0)
                send(one[n])

            def keep(t, carry):
                own[g, t // 2, t % 2] = piece(b1, t // 2, t % 2)
                return carry

            lax.fori_loop(0, 4, keep, 0)

        step = step_of(part, 96)

        def second():
            one[0].wait_recv()
            for n, j in enumerate((1 - b3, b3)):
                def add(at):
                    s2[g, j, at, :] = (own[g, 1 - b2, j, at, :] + r1[g, 1 - b2, j, at, :].astype(F32)).astype(BF16)

                tiled(part, step, add)
                send(two[n])

        def third_step():
            one[1].wait_recv()
            two[0].wait_recv()

            def add(at):
                total = own[g, b2, 1 - b3, at, :] + r1[g, b2, 1 - b3, at, :].astype(F32)
                s3[g, at, :] = (total + r2[g, 1 - b3, at, :].astype(F32)).astype(BF16)

            tiled(part, step, add)
            send(three)

        def fourth():
            two[1].wait_recv()
            three.wait_recv()

            def add(at):
                total = own[g, b2, b3, at, :] + r1[g, b2, b3, at, :].astype(F32)
                total = total + r2[g, b3, at, :].astype(F32) + r3[g, at, :].astype(F32)
                if more:
                    hs[g, 0, at, :] = total.astype(BF16)
                else:
                    got[g, bit["y"], bit["l"], at, :] = total.astype(BF16)

            tiled(part, step, add)
            if more:
                send(more[0])

        def fifth():
            for n in range(len(more)):
                more[n].wait_recv()
                last = n + 1 == len(more)

                def add(at):
                    total = (hs[g, n, at, :].astype(F32) + hr[g, n, at, :].astype(F32)).astype(BF16)
                    if last:
                        got[g, bit["y"], bit["l"], at, :] = total
                    else:
                        hs[g, n + 1, at, :] = total

                tiled(part, step, add)
                if not last:
                    send(more[n + 1])
            send(up1)
            send(up2)

        def sixth():
            up1.wait_recv()
            send(up3)

        def seventh():
            up2.wait_recv()
            up3.wait_recv()
            for a in range(2):
                for b in range(2):
                    out = grads.at[2 * a + b, :, pl.ds(g * wide, wide)]
                    put(local(got.at[g, a, b], out, out_sem.at[g, 2 * a + b]))

        names = dict(T=theirs, O=ours, C2=second, C3=third_step, C4=fourth, C5=fifth, C6=sixth, C7=seventh)
        for name, task in names.items():
            tasks[f"{name}{g}"] = task

    written = []

    def put(copy):
        copy.start()
        written.append(copy)

    for g in range(groups):
        group_tasks(g)

    def matmuls(index, first):
        base = pl.multiple_of(index * rows, 128)

        def key_part(t, carry):
            at = pl.ds(pl.multiple_of(t * 256, 256), 256)
            total = jnp.dot(normed[:, pl.ds(base, rows)], full[index, :, at], preferred_element_type=F32)
            if first:
                kacc[:, at] = total
            else:
                kacc[:, at] += total
            return carry

        lax.fori_loop(0, width // 256, key_part, 0)
        cut = 384

        def back_part(t, carry):
            at = pl.ds(pl.multiple_of(t * cut, 128), cut)
            to = pl.ds(pl.multiple_of(base + t * cut, 128), cut)
            dn[:, to] = lax.dot_general(
                kg[...], full[index, at, :], (((1,), (1,)), ((), ())), preferred_element_type=F32
            )
            return carry

        lax.fori_loop(0, rows // cut, back_part, 0)

    def mo():
        matmuls(shard, True)

    def mc():
        own_copy.wait_recv()
        matmuls(near, False)

    def mf():
        matmuls(far, False)

    def mg():
        for n in range(len(HELPERS)):
            parts[n]["wc"].wait_recv()
            parts[n]["wd"].wait_recv()
        matmuls(both, False)

    tasks.update(MO=mo, MC=mc, MF=mf, MG=mg)

    def finish():
        flat = jnp.concatenate([gains[k : k + 1, :] for k in range(features // gains.shape[1])], axis=1)
        for n in range(3):
            def run(i, carry):
                at = pl.ds(pl.multiple_of(n * third + i * 16, 16), 16)
                kout[at, :] = kacc[at, :].astype(BF16)
                value = x[at, :].astype(F32)
                inv = invs[at, :]
                scaled = dn[at, :] * flat
                inner = jnp.mean(scaled * value, axis=1, keepdims=True)
                tg[at, :] = (inv * scaled - value * (inv * inv * inv * inner)).astype(BF16)
                return carry

            lax.fori_loop(0, third // 16, run, 0)
            at = pl.ds(n * third, third)
            put(local(tg.at[at], token_grad.at[at], out_sem.at[groups, n]))
        put(local(kout, keys, out_sem.at[groups, 3]))

    tasks["FIN"] = finish

    assert sorted(ORDER) == sorted(tasks)
    for name in ORDER:
        tasks[name]()
    for copy in written:
        copy.wait()
    for copy in sent:
        copy.wait_send()


def layer(counts, tokens, gain, key_grad, weight):
    count, features = tokens.shape
    width = key_grad.shape[1]
    rows = weight.shape[0]
    groups = len(HALVES)
    wide = width // groups
    part = rows // 4
    extra = max(bits_of(counts["rep"]) - 2, 1)
    lanes = 128
    any_space = pl.BlockSpec(memory_space=pl.ANY)
    dma = pltpu.SemaphoreType.DMA
    helpers = len(HELPERS)
    scratch = [
        pltpu.VMEM((count, features), BF16),
        pltpu.VMEM((features // lanes, lanes), F32),
        pltpu.VMEM((count, width), BF16),
        pltpu.VMEM((count, features), BF16),
        pltpu.VMEM((features, count), BF16),
        pltpu.VMEM((4, rows, width), BF16),
        pltpu.VMEM((groups, 2, 2, part, wide), F32),
        pltpu.VMEM((groups, 2, 4, part, wide), BF16),
        pltpu.VMEM((groups, 2, 4, part, wide), BF16),
        pltpu.VMEM((groups, 2, 2, part, wide), BF16),
        pltpu.VMEM((groups, 2, 2, part, wide), BF16),
        pltpu.VMEM((groups, 2, part, wide), BF16),
        pltpu.VMEM((groups, 2, part, wide), BF16),
        pltpu.VMEM((groups, part, wide), BF16),
        pltpu.VMEM((groups, part, wide), BF16),
        pltpu.VMEM((groups, extra, part, wide), BF16),
        pltpu.VMEM((groups, extra, part, wide), BF16),
        pltpu.VMEM((groups, 2, 2, part, wide), BF16),
        pltpu.VMEM((count, width), F32),
        pltpu.VMEM((count, features), F32),
        pltpu.VMEM((count, features), BF16),
        pltpu.VMEM((count, width), BF16),
        pltpu.VMEM((count, 1), F32),
        dma((6,)),
        dma((groups + 1, 4)),
        dma((groups, 2)),
        dma((groups, 2, 2)),
        dma((groups, 2, 2)),
        dma((groups, 2)),
        dma((groups, extra, 2)),
        dma((groups, 3, 2)),
        dma((helpers, 2, 2)),
        dma((helpers, 2, 2)),
        dma((2,)),
    ]
    keys, token_grad, grads = pl.pallas_call(
        functools.partial(layer_kernel, counts),
        in_specs=[any_space] * 4,
        out_specs=[any_space] * 3,
        out_shape=[
            jax.ShapeDtypeStruct((count, width), BF16),
            jax.ShapeDtypeStruct((count, features), BF16),
            jax.ShapeDtypeStruct((4, part, width), BF16),
        ],
        scratch_shapes=scratch,
        compiler_params=pltpu.CompilerParams(
            collective_id=0, has_side_effects=True, vmem_limit_bytes=67043328
        ),
        name="layer",
    )(tokens, gain.reshape(features // lanes, lanes), key_grad, weight)
    return keys, token_grad, grads.reshape(rows, width)


def requantize_kernel(chunks, grads, m_code, m_exp, v_code, v_exp, step, m_rel, m_scale, v_rel, v_scale):
    size = m_code.shape[1] // chunks
    units = jnp.concatenate(
        [jnp.exp2(m_exp[...].astype(F32)) / 127.0, jnp.exp2(v_exp[...].astype(F32)) / 255.0], axis=0
    ).T
    tops = []
    for c in range(chunks):
        cols = slice(c * size, (c + 1) * size)
        g = grads[:, cols].astype(F32)
        m_old = m_code[:, cols].astype(F32) * units[:, c : c + 1]
        v_old = v_code[:, cols].astype(F32) * units[:, chunks + c : chunks + c + 1]
        m_new = 0.9 * m_old + 0.1 * g
        v_new = 0.999 * v_old + 0.001 * g * g
        step[:, cols] = (m_new * (1.0 / bias_first)) / (jnp.sqrt(v_new * (1.0 / bias_second)) + 1e-08)
        m_top = jnp.max(jnp.abs(m_new), axis=1, keepdims=True)
        v_top = jnp.max(v_new, axis=1, keepdims=True)
        tops.append((m_top, v_top))
        m_rel[:, cols] = (m_new * (1.0 / (m_top + 1e-06))).astype(BF16)
        v_rel[:, cols] = (v_new * (1.0 / (v_top + 1e-06))).astype(BF16)
    turned = jnp.concatenate([m for m, _ in tops] + [v for _, v in tops], axis=1).T
    m_scale[...] = turned[:chunks]
    v_scale[...] = turned[chunks:]


def requantize(grads, m_code, m_exp, v_code, v_exp):
    rows, width = m_code.shape
    chunks = m_exp.shape[1]
    block = 128
    wide = pl.BlockSpec((block, width), lambda i: (i, 0))
    thin = pl.BlockSpec((chunks, block), lambda i: (0, i))
    shape = jax.ShapeDtypeStruct
    step, m_rel, m_scale, v_rel, v_scale = pl.pallas_call(
        functools.partial(requantize_kernel, chunks),
        grid=(rows // block,),
        in_specs=[wide, wide, thin, wide, thin],
        out_specs=[wide, wide, thin, wide, thin],
        out_shape=[
            shape((rows, width), F32),
            shape((rows, width), BF16),
            shape((chunks, rows), F32),
            shape((rows, width), BF16),
            shape((chunks, rows), F32),
        ],
        name="requantize",
    )(grads, m_code, m_exp.T, v_code, v_exp.T)
    return step, m_rel, m_scale.T, v_rel, v_scale.T


def body(counts, tokens, norm_gain, key_grad, key_weight, m_code, m_exp, v_code, v_exp):
    keys, token_grad, grads = layer(counts, tokens, norm_gain, key_grad, key_weight)
    return (keys, token_grad, *requantize(grads, m_code, m_exp, v_code, v_exp))


def solution(mesh):
    rows = P("shard", None)
    tokens = P(("shard", "rep"), None)
    return jax.shard_map(
        functools.partial(body, dict(mesh.shape)),
        mesh=mesh,
        in_specs=(tokens, P(), tokens, rows, rows, rows, rows, rows),
        out_specs=(tokens, tokens, rows, rows, rows, rows, rows),
        check_vma=False,
    )
```

profile of v0, /device:TPU:0, one launch (start us, length us, event | category | flops | bytes accessed | tf_op | source)
XLA Modules:
  0.0 131.4 jit_solution(17259061971390516189)
XLA Ops:
  0.6 114.2 %layer.1 = (bf16[384,1024]{1,0:T(8,128)(2,1)}, bf16[384,4608]{1,0:T(8,128)(2,1)}, bf16[4,288,1024]{2,1,0:T(8,128)(2,1)}) custom-call(bf16[384,4608]{1,0:T(8,128)(2,1)} %tokens.1, f32[36,128]{1,0:T(8,128)} %bitcast.7, bf16[384,1024]{1,0:T(8,128)(2,1)} %key_grad.1, bf16[1152,1024]{1,0:T(8,128)(2,1)} %weight.1), custom_call_target="tpu_custom_call" | custom-call | tf_op jit(solution)/shard_map/layer/pallas_call | solution.py:443
  114.9 0.0 copy-start
  114.9 12.7 %requantize.1 = (f32[1152,1024]{1,0:T(8,128)}, bf16[1152,1024]{1,0:T(8,128)(2,1)}, f32[4,1152]{1,0:T(4,128)}, bf16[1152,1024]{1,0:T(8,128)(2,1)}, f32[4,1152]{1,0:T(4,128)}) custom-call(bf16[1152,1024]{1,0:T(8,128)(2,1)} %bitcast.6, bf16[1152,1024]{1,0:T(8,128)(2,1)} %m_code.1, s32[4,1152]{1,0:T(4,128)} %bitcast.8, bf16[1152,1024]{1,0:T(8,128)(2,1)} %v_code.1, ...), custom_call_target="tpu_custom_call" | custom-call | tf_op jit(solution)/shard_map/requantize/pallas_call | solution.py:492
  127.5 2.1 %copy.17 = bf16[384,1024]{1,0:T(8,128)(2,1)} copy(bf16[384,1024]{1,0:T(8,128)(2,1)} %get-tuple-element.30) | data formatting | bytes 1572864
  129.6 0.0 copy-done
  129.6 1.8 %copy.18 = bf16[384,4608]{1,0:T(8,128)(2,1)} copy(bf16[384,4608]{1,0:T(8,128)(2,1)S(1)} %copy-done) | data formatting | bytes 7077888
Async XLA Ops:
  114.9 14.7 %copy-start = (bf16[384,4608]{1,0:T(8,128)(2,1)S(1)}, bf16[384,4608]{1,0:T(8,128)(2,1)}, u32[]{:S(2)}) copy-start(bf16[384,4608]{1,0:T(8,128)(2,1)} %get-tuple-element.31) | copy-start | bytes 10616836
where the time goes:
time: 132 us; the launch traced here: 131 us
  Pallas kernels  127 us (96%)
  local copies, waits for them, and re-layouts  3.86 us (3%)
    pallas_call x1, Pallas kernels, layer(): pl.pallas_call(functools.partial(layer_kernel, counts), in_specs=[any_spa...  114 us
    pallas_call x1, Pallas kernels, requantize(): pl.pallas_call(functools.partial(requantize_kernel, chunks), grid=(rows /...  12.7 us
    unnamed x4, local copies, waits for them, and re-layouts  3.86 us

commit v1 on v0

v1 whole, which is shorter than its diff:
```python
import functools

import jax
import jax.numpy as jnp
from jax import lax
from jax.experimental import pallas as pl
from jax.experimental.pallas import tpu as pltpu
from jax.sharding import PartitionSpec as P

bias_first = 0.9999734386011124
bias_second = 0.0952078528862904
F32 = jnp.float32
BF16 = jnp.bfloat16

HALVES = [("x", "y"), ("y", "x"), ("x", "y"), ("y", "x")]
SPREADS = [2, 2, 4]
ORDER = [
    "N0", "GATE", "WX0", "WC", "N1", "N2", "WX2", "RT", "KO", "T1", "T0", "RO", "T3", "WF0", "O1", "O0", "C210",
    "KC", "WF2", "C201", "C200", "BC", "WX1", "C301", "QA2", "O3", "QB2", "T2", "BO", "C310", "C300", "QC2",
    "O2", "QE2", "C401", "C410", "C501", "C400", "C211", "WF1", "C220", "QD2", "C230", "WG0", "C221", "C320",
    "C510", "C420", "C321", "E501", "C500", "E510", "WG1", "C421", "C520", "C311", "C231", "C411", "C521", "KG",
    "C330", "E500", "C331", "C430", "E520", "C511", "KF", "C431", "C530", "E521", "C70", "BF", "E511", "C531",
    "BG", "F0", "E530", "F1", "E531", "C71", "C72", "F2", "C73",
]


def bits_of(count):
    bits = count.bit_length() - 1
    assert 1 << bits == count
    return bits


class Labels:
    def __init__(self, counts):
        shards, reps = bits_of(counts["shard"]), bits_of(counts["rep"])
        assert shards == 2 and reps >= 3
        self.me = {axis: lax.axis_index(axis) for axis in ("shard", "rep")}
        self.of = {"c": ("shard", 0), "x": ("shard", 1), "y": ("rep", 0), "l": ("rep", 1)}
        self.extra = [f"h{n}" for n in range(3, reps)]
        for n in range(3, reps):
            self.of[f"h{n}"] = ("rep", n)
        self.bit = {label: self.digit(axis, 1 << n, 2) for label, (axis, n) in self.of.items()}
        self.place = self.digit("rep", 2, 4)
        self.inner = lax.rem(lax.div(self.place + 1, jnp.int32(2)), jnp.int32(2)) == 1

    def digit(self, axis, unit, base):
        return lax.rem(lax.div(self.me[axis], jnp.int32(unit)), jnp.int32(base))

    def device(self, label):
        if label == "m":
            return {"rep": self.me["rep"] + 2 * (3 - 2 * self.place)}
        axis, n = self.of[label]
        return {axis: self.me[axis] + (1 << n) - 2 * (1 << n) * self.bit[label]}


def tiled(rows, step, body):
    def run(i, carry):
        body(pl.ds(pl.multiple_of(i * step, step), step))
        return carry

    lax.fori_loop(0, rows // step, run, 0)


def step_of(rows, most):
    for step in range(most, 0, -1):
        if rows % step == 0 and step % 16 == 0:
            return step
    return rows


def layer_kernel(counts, tokens, gain, key_grad, weight, keys, token_grad, grads, *scratch):
    (x, gains, kg, normed, turned, full, own, th, kc, s1, r1, s2, r2, zs, zr, hs, hr, got, kacc, dn, kout, invs, flat,
     load_sem, out_sem, core_sem, one_sem, two_sem, low_sem, mid_sem, up_sem, a_sem, wx_sem, wl_sem, wm_sem, wc_sem,
     wo_sem) = scratch
    lab = Labels(counts)
    bit = lab.bit
    tokens_here, features = x.shape
    groups, _, _, part, wide = own.shape
    rows = 4 * part
    width = kg.shape[1]
    shard = lab.me["shard"]
    core = bit["c"]
    unit = rows // 8
    inner = lab.inner

    def local(src, dst, sem):
        return pltpu.make_async_copy(src, dst, sem)

    def remote(src, dst, sems, label):
        return pltpu.make_async_remote_copy(
            src_ref=src, dst_ref=dst, send_sem=sems.at[0], recv_sem=sems.at[1],
            device_id=lab.device(label), device_id_type=pl.DeviceIdType.MESH,
        )

    sent = []

    def send(copy, role=None):
        copy.start()
        sent.append((role, copy))

    loaded = []

    def once(load):
        if all(load is not other for other in loaded):
            loaded.append(load)
            load.wait()

    def only(role):
        return pl.when(inner if role == "inner" else jnp.logical_not(inner))

    third = tokens_here // 3
    loads = [local(tokens.at[pl.ds(n * third, third)], x.at[pl.ds(n * third, third)], load_sem.at[n]) for n in range(3)]
    load_gain = local(gain, gains, load_sem.at[3])
    load_kg = local(key_grad, kg, load_sem.at[4])
    load_w = local(weight, full.at[shard], load_sem.at[5])
    load_gain.start()
    for load in loads:
        load.start()
    load_kg.start()
    load_w.start()

    barrier = pltpu.get_barrier_semaphore()
    greeted = [*lab.of, "m"]
    for label in greeted:
        pl.semaphore_signal(barrier, inc=1, device_id=lab.device(label), device_id_type=pl.DeviceIdType.MESH)
    far = shard + 2 - 4 * bit["x"]
    near = shard + 1 - 2 * core
    both = far + 1 - 2 * core

    def rows_at(place):
        return (2 * place["x"] + place["c"]) * rows + (2 * place["y"] + place["l"]) * part

    tasks = {}

    arrived = []

    def weight_task(n, first, count):
        def at(place):
            return pl.ds(pl.multiple_of((first + place) * unit, 16), unit)

        def move(place, sems, label, shard_at=far):
            ref = full.at[shard_at, at(place)]
            return remote(ref, ref, sems, label)

        place = bit["l"] if count == 2 else lab.place
        beside = place + 1 - 2 * bit["l"]
        across, beyond = 3 - place, 3 - beside
        start = remote(weight.at[at(place)], full.at[shard, at(place)], wx_sem.at[n], "x")
        low = move(place, wl_sem.at[n, 0], "l")
        core0 = move(place, wc_sem.at[n, 0], "c")
        core1 = move(beside, wc_sem.at[n, 1], "c")
        arrived.extend([core0, core1])

        def wx():
            send(start)

        tasks[f"WX{n}"] = wx
        if count == 2:
            def wf():
                start.wait_recv()
                send(low)
                send(core0)

            def wg():
                low.wait_recv()
                send(core1)

            tasks[f"WF{n}"], tasks[f"WG{n}"] = wf, wg
            return

        mid0, mid1 = move(place, wm_sem.at[n, 0], "m"), move(beside, wm_sem.at[n, 1], "m")
        up1, up2 = move(across, wl_sem.at[n, 1], "l"), move(beyond, wl_sem.at[n, 2], "l")
        core_a, core_b = move(across, wc_sem.at[n, 2], "c"), move(beyond, wc_sem.at[n, 3], "c")
        end_a, end_b = move(beyond, wc_sem.at[n, 2], "c"), move(across, wc_sem.at[n, 3], "c")
        arrived.extend([core_a, core_b])

        def wf():
            start.wait_recv()
            send(low)

            @only("inner")
            def _():
                send(mid0, "inner")

            send(core0)

        def qa():
            low.wait_recv()

            @only("inner")
            def _():
                send(mid1, "inner")

            send(core1)

        def qb():
            @only("inner")
            def _():
                mid0.wait_recv()
                send(up1, "inner")
                send(core_a, "inner")

        def qc():
            @only("inner")
            def _():
                mid1.wait_recv()
                send(up2, "inner")
                send(core_b, "inner")

        def qd():
            @only("outer")
            def _():
                up1.wait_recv()
                send(end_a, "outer")

        def qe():
            @only("outer")
            def _():
                up2.wait_recv()
                send(end_b, "outer")

        for name, task in dict(WF=wf, QA=qa, QB=qb, QC=qc, QD=qd, QE=qe).items():
            tasks[f"{name}{n}"] = task

    first = 0
    for n, count in enumerate(SPREADS):
        weight_task(n, first, count)
        first += count
    assert first == 8
    own_copy = remote(full.at[shard], full.at[shard], wo_sem, "c")

    def weight_core():
        once(load_w)
        send(own_copy)

    tasks["WC"] = weight_core

    def gate():
        pl.semaphore_wait(barrier, len(greeted))

    tasks["GATE"] = gate

    def norm_task(n):
        def norm():
            if n == 0:
                load_gain.wait()
                flat[...] = jnp.concatenate([gains[k : k + 1, :] for k in range(features // gains.shape[1])], axis=1)
            loads[n].wait()

            def run(i, carry):
                at = pl.ds(pl.multiple_of(n * third + i * 16, 16), 16)
                value = x[at, :].astype(F32)
                inv = lax.rsqrt(jnp.mean(value * value, axis=1, keepdims=True) + 1e-06)
                invs[at, :] = inv
                normed[at, :] = (value * inv * flat[...]).astype(BF16)
                return carry

            lax.fori_loop(0, third // 16, run, 0, unroll=4)

        tasks[f"N{n}"] = norm

    def turn_task(name, half):
        def turn():
            for a in range(2):
                base = (2 * a + half) * rows

                def run(i, carry):
                    at = pl.ds(pl.multiple_of(base + i * 128, 128), 128)
                    turned[at, :] = normed[:, at].T
                    return carry

                lax.fori_loop(0, rows // 128, run, 0, unroll=3)

        tasks[name] = turn

    turn_task("RT", 1 - core)
    turn_task("RO", core)
    for n in range(3):
        norm_task(n)

    def outer(place, g):
        start = (2 * place["x"] + place["c"]) * rows + (2 * place["y"] + place["k"]) * part
        at = pl.ds(pl.multiple_of(start, 16), part)
        return jnp.dot(turned[at, :], kg[:, g * wide : (g + 1) * wide], preferred_element_type=F32)

    core_copies = [remote(th.at[g], kc.at[g], core_sem.at[g], "c") for g in range(groups)]

    def group_tasks(g):
        o1, o2 = HALVES[g]
        b1, b2 = bit[o1], bit[o2]
        def theirs():
            once(load_kg)

            def run(t, carry):
                a, b = t // 2, t % 2
                start = (2 * a + 1 - core) * rows + b * 2 * part
                at = pl.ds(pl.multiple_of(start, 16), 2 * part)
                total = jnp.dot(turned[at, :], kg[:, g * wide : (g + 1) * wide], preferred_element_type=F32)
                th[g, a, 2 * b] = total[:part].astype(BF16)
                th[g, a, 2 * b + 1] = total[part:].astype(BF16)
                return carry

            lax.fori_loop(0, 4, run, 0, unroll=2)
            send(core_copies[g])

        one = [[remote(s1.at[g, j, k], r1.at[g, j, k], one_sem.at[g, n, k], o1) for k in range(2)] for n, j in enumerate((1 - b2, b2))]

        def ours():
            core_copies[g].wait_recv()

            def piece(first, second, k):
                place = {o1: first, o2: second, "k": k, "c": core}
                came = kc[g, place["x"], 2 * place["y"] + k]
                return outer(place, g) + came.astype(F32)

            for n, j in enumerate((1 - b2, b2)):
                for k in range(2):
                    s1[g, j, k] = piece(1 - b1, j, k).astype(BF16)
                for k in range(2):
                    send(one[n][k])

            def keep(t, carry):
                own[g, t // 2, t % 2] = piece(b1, t // 2, t % 2)
                return carry

            lax.fori_loop(0, 4, keep, 0, unroll=2)

        tasks[f"T{g}"], tasks[f"O{g}"] = theirs, ours
        step = step_of(part, 96)
        arrivals = []

        def half_tasks(k):
            two = remote(s2.at[g, k], r2.at[g, k], two_sem.at[g, k], o2)
            low = remote(zs.at[g, k], zr.at[g, k], low_sem.at[g, k], "l")
            lanes = ["m", *lab.extra]
            mids = [remote(hs.at[g, k, n], hr.at[g, k, n], mid_sem.at[g, k, n], label) for n, label in enumerate(lanes)]
            mine = got.at[g, bit["y"], k]
            up = remote(mine, mine, up_sem.at[g, k], "l")
            last = remote(mine, mine, a_sem.at[g, k], "y")
            arrivals.append(last)

            def second():
                one[0][k].wait_recv()

                def add(at):
                    s2[g, k, at, :] = (own[g, 1 - b2, k, at, :] + r1[g, 1 - b2, k, at, :].astype(F32)).astype(BF16)

                tiled(part, step, add)
                send(two)

            def total(at):
                value = own[g, b2, k, at, :] + r1[g, b2, k, at, :].astype(F32)
                return value + r2[g, k, at, :].astype(F32)

            def third_step():
                @only("outer")
                def _():
                    one[1][k].wait_recv()
                    two.wait_recv()

                    def add(at):
                        zs[g, k, at, :] = total(at).astype(BF16)

                    tiled(part, step, add)
                    send(low, "outer")

            def fourth():
                @only("inner")
                def _():
                    one[1][k].wait_recv()
                    two.wait_recv()
                    low.wait_recv()

                    def add(at):
                        hs[g, k, 0, at, :] = (total(at) + zr[g, k, at, :].astype(F32)).astype(BF16)

                    tiled(part, step, add)
                    send(mids[0], "inner")

            def fifth():
                @only("inner")
                def _():
                    for n in range(len(mids)):
                        mids[n].wait_recv()

                        def add(at):
                            value = (hs[g, k, n, at, :].astype(F32) + hr[g, k, n, at, :].astype(F32)).astype(BF16)
                            if n + 1 == len(mids):
                                got[g, bit["y"], k, at, :] = value
                            else:
                                hs[g, k, n + 1, at, :] = value

                        tiled(part, step, add)
                        if n + 1 < len(mids):
                            send(mids[n + 1], "inner")
                    send(up, "inner")
                    send(last, "inner")

            def ends():
                @only("outer")
                def _():
                    up.wait_recv()
                    send(last, "outer")

            for name, task in dict(C2=second, C3=third_step, C4=fourth, C5=fifth, E5=ends).items():
                tasks[f"{name}{g}{k}"] = task

        for k in range(2):
            half_tasks(k)

        def seventh():
            for copy in arrivals:
                copy.wait_recv()
            for a in range(2):
                for k in range(2):
                    out = grads.at[2 * a + k, :, pl.ds(g * wide, wide)]
                    put(local(got.at[g, a, k], out, out_sem.at[g, 2 * a + k]))

        tasks[f"C7{g}"] = seventh

    written = []

    def put(copy):
        copy.start()
        written.append(copy)

    for g in range(groups):
        group_tasks(g)

    def forward(index, first):
        base = pl.multiple_of(index * rows, 128)

        def key_part(t, carry):
            at = pl.ds(pl.multiple_of(t * 256, 256), 256)
            total = jnp.dot(normed[:, pl.ds(base, rows)], full[index, :, at], preferred_element_type=F32)
            if first:
                kacc[:, at] = total
            else:
                kacc[:, at] += total
            return carry

        lax.fori_loop(0, width // 256, key_part, 0, unroll=2)

    def backward(index):
        base = pl.multiple_of(index * rows, 128)
        cut = 384

        def back_part(t, carry):
            at = pl.ds(pl.multiple_of(t * cut, 128), cut)
            to = pl.ds(pl.multiple_of(base + t * cut, 128), cut)
            dn[:, to] = lax.dot_general(
                kg[...], full[index, at, :], (((1,), (1,)), ((), ())), preferred_element_type=F32
            )
            return carry

        lax.fori_loop(0, rows // cut, back_part, 0)

    def own_forward():
        once(load_w)
        forward(shard, True)

    def own_backward():
        once(load_w)
        once(load_kg)
        backward(shard)

    def near_forward():
        own_copy.wait_recv()
        forward(near, False)

    def both_forward():
        for copy in arrived:
            copy.wait_recv()
        forward(both, False)

    tasks.update(
        KO=own_forward, BO=own_backward,
        KC=near_forward, BC=lambda: backward(near),
        KF=lambda: forward(far, False), BF=lambda: backward(far),
        KG=both_forward, BG=lambda: backward(both),
    )

    def finish_task(n):
        def finish():
            def run(i, carry):
                at = pl.ds(pl.multiple_of(n * third + i * 16, 16), 16)
                kout[at, :] = kacc[at, :].astype(BF16)
                value = x[at, :].astype(F32)
                inv = invs[at, :]
                scaled = dn[at, :] * flat[...]
                inner = jnp.mean(scaled * value, axis=1, keepdims=True)
                x[at, :] = (inv * scaled - value * (inv * inv * inv * inner)).astype(BF16)
                return carry

            lax.fori_loop(0, third // 16, run, 0, unroll=2)
            at = pl.ds(n * third, third)
            put(local(x.at[at], token_grad.at[at], out_sem.at[groups, n]))
            if n == 2:
                put(local(kout, keys, out_sem.at[groups, 3]))

        tasks[f"F{n}"] = finish

    for n in range(3):
        finish_task(n)

    assert sorted(ORDER) == sorted(tasks)
    for name in ORDER:
        tasks[name]()
    for copy in written:
        copy.wait()
    for role, copy in sent:
        if role is None:
            copy.wait_send()
    for role in ("inner", "outer"):
        @only(role)
        def _():
            for where, copy in sent:
                if where == role:
                    copy.wait_send()


def layer(counts, tokens, gain, key_grad, weight):
    count, features = tokens.shape
    width = key_grad.shape[1]
    rows = weight.shape[0]
    groups = len(HALVES)
    wide = width // groups
    part = rows // 4
    hops = 1 + bits_of(counts["rep"]) - 3
    lanes = 128
    any_space = pl.BlockSpec(memory_space=pl.ANY)
    dma = pltpu.SemaphoreType.DMA
    spreads = len(SPREADS)
    scratch = [
        pltpu.VMEM((count, features), BF16),
        pltpu.VMEM((features // lanes, lanes), F32),
        pltpu.VMEM((count, width), BF16),
        pltpu.VMEM((count, features), BF16),
        pltpu.VMEM((features, count), BF16),
        pltpu.VMEM((4, rows, width), BF16),
        pltpu.VMEM((groups, 2, 2, part, wide), F32),
        pltpu.VMEM((groups, 2, 4, part, wide), BF16),
        pltpu.VMEM((groups, 2, 4, part, wide), BF16),
        pltpu.VMEM((groups, 2, 2, part, wide), BF16),
        pltpu.VMEM((groups, 2, 2, part, wide), BF16),
        pltpu.VMEM((groups, 2, part, wide), BF16),
        pltpu.VMEM((groups, 2, part, wide), BF16),
        pltpu.VMEM((groups, 2, part, wide), BF16),
        pltpu.VMEM((groups, 2, part, wide), BF16),
        pltpu.VMEM((groups, 2, hops, part, wide), BF16),
        pltpu.VMEM((groups, 2, hops, part, wide), BF16),
        pltpu.VMEM((groups, 2, 2, part, wide), BF16),
        pltpu.VMEM((count, width), F32),
        pltpu.VMEM((count, features), F32),
        pltpu.VMEM((count, width), BF16),
        pltpu.VMEM((count, 1), F32),
        pltpu.VMEM((1, features), F32),
        dma((6,)),
        dma((groups + 1, 4)),
        dma((groups, 2)),
        dma((groups, 2, 2, 2)),
        dma((groups, 2, 2)),
        dma((groups, 2, 2)),
        dma((groups, 2, hops, 2)),
        dma((groups, 2, 2)),
        dma((groups, 2, 2)),
        dma((spreads, 2)),
        dma((spreads, 3, 2)),
        dma((spreads, 2, 2)),
        dma((spreads, 4, 2)),
        dma((2,)),
    ]
    keys, token_grad, grads = pl.pallas_call(
        functools.partial(layer_kernel, counts),
        in_specs=[any_space] * 4,
        out_specs=[any_space] * 3,
        out_shape=[
            jax.ShapeDtypeStruct((count, width), BF16),
            jax.ShapeDtypeStruct((count, features), BF16),
            jax.ShapeDtypeStruct((4, part, width), BF16),
        ],
        scratch_shapes=scratch,
        compiler_params=pltpu.CompilerParams(
            collective_id=0, has_side_effects=True, vmem_limit_bytes=67043328
        ),
        name="layer",
    )(tokens, gain.reshape(features // lanes, lanes), key_grad, weight)
    return keys, token_grad, grads.reshape(rows, width)


def requantize_kernel(
    chunks, sub, grads, m_code, m_exp, v_code, v_exp, keys_in, token_in,
    step, m_rel, m_scale, v_rel, v_scale, keys_out, token_out,
    units, tops, keys, token, sems,
):
    here, last = pl.program_id(0), pl.num_programs(0) - 1
    into = [pltpu.make_async_copy(token_in, token, sems.at[0]), pltpu.make_async_copy(keys_in, keys, sems.at[1])]
    back = [pltpu.make_async_copy(token, token_out, sems.at[2]), pltpu.make_async_copy(keys, keys_out, sems.at[3])]

    @pl.when(here == 0)
    def _():
        for copy in into:
            copy.start()

    rows, width = m_code.shape
    size = width // chunks
    unit_m = jnp.exp2(m_exp[...].astype(F32)) * (0.9 / 127.0)
    unit_v = jnp.exp2(v_exp[...].astype(F32)) * (0.999 / 255.0)
    units[...] = jnp.concatenate([unit_m, unit_v], axis=0).T
    floor = 1e-08 * bias_second**0.5
    rate = bias_second**0.5 / bias_first

    def run(i, carry):
        at = pl.ds(pl.multiple_of(i * sub, sub), sub)
        for c in range(chunks):
            cols = slice(c * size, (c + 1) * size)
            g = grads[at, cols].astype(F32)
            m_new = m_code[at, cols].astype(F32) * units[at, c : c + 1] + 0.1 * g
            v_new = v_code[at, cols].astype(F32) * units[at, chunks + c : chunks + c + 1] + 0.001 * g * g
            root = v_new * lax.rsqrt(v_new)
            step[at, cols] = (m_new * rate) / (root + floor)
            m_top = jnp.max(jnp.abs(m_new), axis=1, keepdims=True)
            v_top = jnp.max(v_new, axis=1, keepdims=True)
            tops[at, c : c + 1] = m_top
            tops[at, chunks + c : chunks + c + 1] = v_top
            m_rel[at, cols] = (m_new * (1.0 / (m_top + 1e-06))).astype(BF16)
            v_rel[at, cols] = (v_new * (1.0 / (v_top + 1e-06))).astype(BF16)
        return carry

    lax.fori_loop(0, rows // sub, run, 0, unroll=True)
    turned = tops[...].T
    m_scale[...] = turned[:chunks]
    v_scale[...] = turned[chunks:]

    @pl.when(here == last - 1)
    def _():
        for one, other in zip(into, back):
            one.wait()
            other.start()

    @pl.when(here == last)
    def _():
        for copy in back:
            copy.wait()


def requantize(grads, m_code, m_exp, v_code, v_exp, keys, token_grad, block=384, sub=128):
    rows, width = m_code.shape
    chunks = m_exp.shape[1]
    wide = pl.BlockSpec((block, width), lambda i: (i, 0))
    thin = pl.BlockSpec((chunks, block), lambda i: (0, i))
    any_space = pl.BlockSpec(memory_space=pl.ANY)
    shape = jax.ShapeDtypeStruct
    step, m_rel, m_scale, v_rel, v_scale, keys, token_grad = pl.pallas_call(
        functools.partial(requantize_kernel, chunks, sub),
        grid=(rows // block,),
        in_specs=[wide, wide, thin, wide, thin, any_space, any_space],
        out_specs=[wide, wide, thin, wide, thin, any_space, any_space],
        out_shape=[
            shape((rows, width), F32),
            shape((rows, width), BF16),
            shape((chunks, rows), F32),
            shape((rows, width), BF16),
            shape((chunks, rows), F32),
            shape(keys.shape, keys.dtype),
            shape(token_grad.shape, token_grad.dtype),
        ],
        scratch_shapes=[
            pltpu.VMEM((block, 2 * chunks), F32),
            pltpu.VMEM((block, 2 * chunks), F32),
            pltpu.VMEM(keys.shape, keys.dtype),
            pltpu.VMEM(token_grad.shape, token_grad.dtype),
            pltpu.SemaphoreType.DMA((4,)),
        ],
        name="requantize",
    )(grads, m_code, m_exp.T, v_code, v_exp.T, keys, token_grad)
    return keys, token_grad, step, m_rel, m_scale.T, v_rel, v_scale.T


def body(counts, tokens, norm_gain, key_grad, key_weight, m_code, m_exp, v_code, v_exp):
    keys, token_grad, grads = layer(counts, tokens, norm_gain, key_grad, key_weight)
    return requantize(grads, m_code, m_exp, v_code, v_exp, keys, token_grad)


def solution(mesh):
    rows = P("shard", None)
    tokens = P(("shard", "rep"), None)
    return jax.shard_map(
        functools.partial(body, dict(mesh.shape)),
        mesh=mesh,
        in_specs=(tokens, P(), tokens, rows, rows, rows, rows, rows),
        out_specs=(tokens, tokens, rows, rows, rows, rows, rows),
        check_vma=False,
    )
```

time: 132 us -> 99.1 us (0.75)
  Pallas kernels: 127 us -> 98.2 us
  local copies, waits for them, and re-layouts: 3.86 us -> 0 us
    pallas_call x1, Pallas kernels: 114 us -> 88.2 us  [layer(): pl.pallas_call(functools.partial(layer_kernel, counts), in_specs=[any_spa...]
    unnamed x4 -> x0, local copies, waits for them, and re-layouts: 3.86 us -> none
    pallas_call x1, Pallas kernels: 12.7 us -> 10 us  [requantize(): pl.pallas_call(functools.partial(requantize_kernel, chunks, sub), grid=(r...]
where the time goes in v1:
time: 99.1 us; the launch traced here: 99 us
  Pallas kernels  98.2 us (99%)
    pallas_call x1, Pallas kernels, layer(): pl.pallas_call(functools.partial(layer_kernel, counts), in_specs=[any_spa...  88.2 us
    pallas_call x1, Pallas kernels, requantize(): pl.pallas_call(functools.partial(requantize_kernel, chunks, sub), grid=(r...  10 us

profile of v1, /device:TPU:0, one launch (start us, length us, event | category | flops | bytes accessed | tf_op | source)
XLA Modules:
  0.0 99.0 jit_solution(10128176831411474211)
XLA Ops:
  0.6 88.2 %layer.1 = (bf16[384,1024]{1,0:T(8,128)(2,1)}, bf16[384,4608]{1,0:T(8,128)(2,1)}, bf16[4,288,1024]{2,1,0:T(8,128)(2,1)}) custom-call(bf16[384,4608]{1,0:T(8,128)(2,1)} %tokens.1, f32[36,128]{1,0:T(8,128)} %bitcast.7, bf16[384,1024]{1,0:T(8,128)(2,1)} %key_grad.1, bf16[1152,1024]{1,0:T(8,128)(2,1)} %weight.1), custom_call_target="tpu_custom_call" | custom-call | tf_op jit(solution)/shard_map/layer/pallas_call | solution.py:573
  88.8 10.0 %requantize.1 = (f32[1152,1024]{1,0:T(8,128)}, bf16[1152,1024]{1,0:T(8,128)(2,1)}, f32[4,1152]{1,0:T(4,128)}, bf16[1152,1024]{1,0:T(8,128)(2,1)}, f32[4,1152]{1,...) custom-call(bf16[1152,1024]{1,0:T(8,128)(2,1)} %bitcast.6, bf16[1152,1024]{1,0:T(8,128)(2,1)} %m_code.1, ...), custom_call_target="tpu_custom_call" | custom-call | tf_op jit(solution)/shard_map/requantize/pallas_call | solution.py:654

commit v2 on v1

--- a/solution.py
+++ b/solution.py
@@ -12,15 +12,23 @@
 F32 = jnp.float32
 BF16 = jnp.bfloat16
 
-HALVES = [("x", "y"), ("y", "x"), ("x", "y"), ("y", "x")]
+GROUPS = 4
+CUTS = 3
+HALVES = [
+    "x", "y", "x", "x", "y", "y", "y", "x", "y", "y", "y", "y",
+]
+KINDS = ["core", "one", "two", "low", "mid", "up", "last", "far"]
 SPREADS = [2, 2, 4]
 ORDER = [
-    "N0", "GATE", "WX0", "WC", "N1", "N2", "WX2", "RT", "KO", "T1", "T0", "RO", "T3", "WF0", "O1", "O0", "C210",
-    "KC", "WF2", "C201", "C200", "BC", "WX1", "C301", "QA2", "O3", "QB2", "T2", "BO", "C310", "C300", "QC2",
-    "O2", "QE2", "C401", "C410", "C501", "C400", "C211", "WF1", "C220", "QD2", "C230", "WG0", "C221", "C320",
-    "C510", "C420", "C321", "E501", "C500", "E510", "WG1", "C421", "C520", "C311", "C231", "C411", "C521", "KG",
-    "C330", "E500", "C331", "C430", "E520", "C511", "KF", "C431", "C530", "E521", "C70", "BF", "E511", "C531",
-    "BG", "F0", "E530", "F1", "E531", "C71", "C72", "F2", "C73",
+    "N0", "N1", "N2", "RT", "GATE", "WX0", "T.8", "T.6", "RO", "T.9", "WX2", "O.8", "T.4", "T.10", "O.9", "T.1",
+    "T.3", "WF0", "T.11", "T.5", "O.11", "WX1", "O.6", "T.7", "T.2", "WF2", "C2.9", "WC", "C2.8", "T.0", "O.1",
+    "WF1", "O.4", "C2.1", "O.3", "QB2", "O.7", "QA2", "BO", "C3.8", "C3.9", "O.5", "C2.3", "C4.8", "C2.5", "KO",
+    "QC2", "C3.1", "O.2", "C2.7", "C3.3", "O.10", "C3.5", "WG0", "C5.8", "C4.1", "KC", "C2.4", "C2.2", "C2.11",
+    "C3.7", "C4.9", "C4.5", "E5.8", "C2.10", "C5.1", "C4.7", "C5.9", "O.0", "QD2", "WG1", "C3.4", "QE2", "E5.1",
+    "C3.2", "C5.5", "E5.9", "C4.3", "C3.11", "BC", "C5.7", "E5.5", "C7.8", "C4.4", "C4.2", "C3.10", "C2.6",
+    "C5.4", "C4.11", "C2.0", "C5.3", "C7.1", "E5.7", "C7.9", "KG", "C4.10", "KF", "C3.0", "C5.11", "E5.4", "BF",
+    "E5.3", "C3.6", "C5.2", "C7.4", "E5.11", "C4.0", "C7.7", "C5.10", "C7.5", "BG", "E5.2", "C4.6", "F0",
+    "C7.3", "E5.10", "C5.0", "F1", "C7.11", "C5.6", "F2", "E5.0", "C7.2", "C7.10", "E5.6", "C7.0", "C7.6",
 ]
 
 
@@ -69,14 +77,14 @@
 
 
 def layer_kernel(counts, tokens, gain, key_grad, weight, keys, token_grad, grads, *scratch):
-    (x, gains, kg, normed, turned, full, own, th, kc, s1, r1, s2, r2, zs, zr, hs, hr, got, kacc, dn, kout, invs, flat,
-     load_sem, out_sem, core_sem, one_sem, two_sem, low_sem, mid_sem, up_sem, a_sem, wx_sem, wl_sem, wm_sem, wc_sem,
+    (x, gains, kg, normed, turned, full, own, th, kc, s1, r1, s2, r2, zr, hs, hr, got, kacc, dn, tg, kout, invs, flat,
+     load_sem, out_sem, part_sem, send_sem, core_sem, one_sem, two_sem, low_sem, mid_sem, up_sem, a_sem, wx_sem, wl_sem, wm_sem, wc_sem,
      wo_sem) = scratch
     lab = Labels(counts)
     bit = lab.bit
     tokens_here, features = x.shape
-    groups, _, _, part, wide = own.shape
-    rows = 4 * part
+    blocks, _, part, wide = own.shape
+    rows = full.shape[1]
     width = kg.shape[1]
     shard = lab.me["shard"]
     core = bit["c"]
@@ -86,17 +94,17 @@
     def local(src, dst, sem):
         return pltpu.make_async_copy(src, dst, sem)
 
-    def remote(src, dst, sems, label):
+    def remote(src, dst, came, label, kind):
         return pltpu.make_async_remote_copy(
-            src_ref=src, dst_ref=dst, send_sem=sems.at[0], recv_sem=sems.at[1],
+            src_ref=src, dst_ref=dst, send_sem=send_sem.at[KINDS.index(kind)], recv_sem=came,
             device_id=lab.device(label), device_id_type=pl.DeviceIdType.MESH,
         )
 
-    sent = []
-
-    def send(copy, role=None):
+    sent = {None: 0, "inner": 0, "outer": 0}
+
+    def send(copy, role=None, units=0):
         copy.start()
-        sent.append((role, copy))
+        sent[role] += units
 
     loaded = []
 
@@ -140,30 +148,30 @@
 
         def move(place, sems, label, shard_at=far):
             ref = full.at[shard_at, at(place)]
-            return remote(ref, ref, sems, label)
+            return remote(ref, ref, sems, label, "far")
 
         place = bit["l"] if count == 2 else lab.place
         beside = place + 1 - 2 * bit["l"]
         across, beyond = 3 - place, 3 - beside
-        start = remote(weight.at[at(place)], full.at[shard, at(place)], wx_sem.at[n], "x")
+        start = remote(weight.at[at(place)], full.at[shard, at(place)], wx_sem.at[n], "x", "far")
         low = move(place, wl_sem.at[n, 0], "l")
         core0 = move(place, wc_sem.at[n, 0], "c")
         core1 = move(beside, wc_sem.at[n, 1], "c")
         arrived.extend([core0, core1])
 
         def wx():
-            send(start)
+            send(start, None, 1)
 
         tasks[f"WX{n}"] = wx
         if count == 2:
             def wf():
                 start.wait_recv()
-                send(low)
-                send(core0)
+                send(low, None, 1)
+                send(core0, None, 1)
 
             def wg():
                 low.wait_recv()
-                send(core1)
+                send(core1, None, 1)
 
             tasks[f"WF{n}"], tasks[f"WG{n}"] = wf, wg
             return
@@ -176,48 +184,48 @@
 
         def wf():
             start.wait_recv()
-            send(low)
+            send(low, None, 1)
 
             @only("inner")
             def _():
-                send(mid0, "inner")
-
-            send(core0)
+                send(mid0, "inner", 1)
+
+            send(core0, None, 1)
 
         def qa():
             low.wait_recv()
 
             @only("inner")
             def _():
-                send(mid1, "inner")
-
-            send(core1)
+                send(mid1, "inner", 1)
+
+            send(core1, None, 1)
 
         def qb():
             @only("inner")
             def _():
                 mid0.wait_recv()
-                send(up1, "inner")
-                send(core_a, "inner")
+                send(up1, "inner", 1)
+                send(core_a, "inner", 1)
 
         def qc():
             @only("inner")
             def _():
                 mid1.wait_recv()
-                send(up2, "inner")
-                send(core_b, "inner")
+                send(up2, "inner", 1)
+                send(core_b, "inner", 1)
 
         def qd():
             @only("outer")
             def _():
                 up1.wait_recv()
-                send(end_a, "outer")
+                send(end_a, "outer", 1)
 
         def qe():
             @only("outer")
             def _():
                 up2.wait_recv()
-                send(end_b, "outer")
+                send(end_b, "outer", 1)
 
         for name, task in dict(WF=wf, QA=qa, QB=qb, QC=qc, QD=qd, QE=qe).items():
             tasks[f"{name}{n}"] = task
@@ -227,11 +235,11 @@
         weight_task(n, first, count)
         first += count
     assert first == 8
-    own_copy = remote(full.at[shard], full.at[shard], wo_sem, "c")
+    own_copy = remote(full.at[shard], full.at[shard], wo_sem.at[0], "c", "far")
 
     def weight_core():
         once(load_w)
-        send(own_copy)
+        send(own_copy, None, 8)
 
     tasks["WC"] = weight_core
 
@@ -278,145 +286,124 @@
     for n in range(3):
         norm_task(n)
 
-    def outer(place, g):
-        start = (2 * place["x"] + place["c"]) * rows + (2 * place["y"] + place["k"]) * part
+    def outer(place, b):
+        g, k = b // CUTS, b % CUTS
+        start = (2 * place["x"] + place["c"]) * rows + (CUTS * place["y"] + k) * part
         at = pl.ds(pl.multiple_of(start, 16), part)
         return jnp.dot(turned[at, :], kg[:, g * wide : (g + 1) * wide], preferred_element_type=F32)
 
-    core_copies = [remote(th.at[g], kc.at[g], core_sem.at[g], "c") for g in range(groups)]
-
-    def group_tasks(g):
-        o1, o2 = HALVES[g]
+    step = step_of(part, 96)
+
+    def block_tasks(b):
+        o1 = HALVES[b]
+        o2 = "y" if o1 == "x" else "x"
         b1, b2 = bit[o1], bit[o2]
+        g, k = b // CUTS, b % CUTS
+        over = remote(th.at[b], kc.at[b], core_sem.at[b], "c", "core")
+        one = [remote(s1.at[b, j], r1.at[b, j], one_sem.at[b, n], o1, "one") for n, j in enumerate((1 - b2, b2))]
+        two = remote(s2.at[b], r2.at[b], two_sem.at[b], o2, "two")
+        low = remote(hs.at[b, 0], zr.at[b], low_sem.at[b], "l", "low")
+        lanes = ["m", *lab.extra]
+        mids = [remote(hs.at[b, n], hr.at[b, n], mid_sem.at[b, n], label, "mid") for n, label in enumerate(lanes)]
+        mine = got.at[b, bit["y"]]
+        up = remote(mine, mine, up_sem.at[b], "l", "up")
+        last = remote(mine, mine, a_sem.at[b], "y", "last")
+
         def theirs():
             once(load_kg)
-
-            def run(t, carry):
-                a, b = t // 2, t % 2
-                start = (2 * a + 1 - core) * rows + b * 2 * part
-                at = pl.ds(pl.multiple_of(start, 16), 2 * part)
-                total = jnp.dot(turned[at, :], kg[:, g * wide : (g + 1) * wide], preferred_element_type=F32)
-                th[g, a, 2 * b] = total[:part].astype(BF16)
-                th[g, a, 2 * b + 1] = total[part:].astype(BF16)
-                return carry
-
-            lax.fori_loop(0, 4, run, 0, unroll=2)
-            send(core_copies[g])
-
-        one = [[remote(s1.at[g, j, k], r1.at[g, j, k], one_sem.at[g, n, k], o1) for k in range(2)] for n, j in enumerate((1 - b2, b2))]
+            for a in range(2):
+                for y in range(2):
+                    th[b, a, y] = outer({"x": a, "y": y, "c": 1 - core}, b).astype(BF16)
+            send(over)
 
         def ours():
-            core_copies[g].wait_recv()
-
-            def piece(first, second, k):
-                place = {o1: first, o2: second, "k": k, "c": core}
-                came = kc[g, place["x"], 2 * place["y"] + k]
-                return outer(place, g) + came.astype(F32)
+            over.wait_recv()
+
+            def piece(first, second):
+                place = {o1: first, o2: second, "c": core}
+                return outer(place, b) + kc[b, place["x"], place["y"]].astype(F32)
 
             for n, j in enumerate((1 - b2, b2)):
-                for k in range(2):
-                    s1[g, j, k] = piece(1 - b1, j, k).astype(BF16)
-                for k in range(2):
-                    send(one[n][k])
-
-            def keep(t, carry):
-                own[g, t // 2, t % 2] = piece(b1, t // 2, t % 2)
-                return carry
-
-            lax.fori_loop(0, 4, keep, 0, unroll=2)
-
-        tasks[f"T{g}"], tasks[f"O{g}"] = theirs, ours
-        step = step_of(part, 96)
-        arrivals = []
-
-        def half_tasks(k):
-            two = remote(s2.at[g, k], r2.at[g, k], two_sem.at[g, k], o2)
-            low = remote(zs.at[g, k], zr.at[g, k], low_sem.at[g, k], "l")
-            lanes = ["m", *lab.extra]
-            mids = [remote(hs.at[g, k, n], hr.at[g, k, n], mid_sem.at[g, k, n], label) for n, label in enumerate(lanes)]
-            mine = got.at[g, bit["y"], k]
-            up = remote(mine, mine, up_sem.at[g, k], "l")
-            last = remote(mine, mine, a_sem.at[g, k], "y")
-            arrivals.append(last)
-
-            def second():
-                one[0][k].wait_recv()
+                s1[b, j] = piece(1 - b1, j).astype(BF16)
+                send(one[n])
+            for j in range(2):
+                own[b, j] = piece(b1, j)
+
+        def second():
+            one[0].wait_recv()
+
+            def add(at):
+                s2[b, at, :] = (own[b, 1 - b2, at, :] + r1[b, 1 - b2, at, :].astype(F32)).astype(BF16)
+
+            tiled(part, step, add)
+            send(two)
+
+        def total(at):
+            value = own[b, b2, at, :] + r1[b, b2, at, :].astype(F32)
+            return value + r2[b, at, :].astype(F32)
+
+        def third_step():
+            @only("outer")
+            def _():
+                one[1].wait_recv()
+                two.wait_recv()
 
                 def add(at):
-                    s2[g, k, at, :] = (own[g, 1 - b2, k, at, :] + r1[g, 1 - b2, k, at, :].astype(F32)).astype(BF16)
+                    hs[b, 0, at, :] = total(at).astype(BF16)
 
                 tiled(part, step, add)
-                send(two)
-
-            def total(at):
-                value = own[g, b2, k, at, :] + r1[g, b2, k, at, :].astype(F32)
-                return value + r2[g, k, at, :].astype(F32)
-
-            def third_step():
-                @only("outer")
-                def _():
-                    one[1][k].wait_recv()
-                    two.wait_recv()
+                send(low, "outer")
+
+        def fourth():
+            @only("inner")
+            def _():
+                one[1].wait_recv()
+                two.wait_recv()
+                low.wait_recv()
+
+                def add(at):
+                    hs[b, 0, at, :] = (total(at) + zr[b, at, :].astype(F32)).astype(BF16)
+
+                tiled(part, step, add)
+                send(mids[0], "inner")
+
+        def fifth():
+            @only("inner")
+            def _():
+                for n in range(len(mids)):
+                    mids[n].wait_recv()
 
                     def add(at):
-                        zs[g, k, at, :] = total(at).astype(BF16)
+                        value = (hs[b, n, at, :].astype(F32) + hr[b, n, at, :].astype(F32)).astype(BF16)
+                        if n + 1 == len(mids):
+                            got[b, bit["y"], at, :] = value
+                        else:
+                            hs[b, n + 1, at, :] = value
 
                     tiled(part, step, add)
-                    send(low, "outer")
-
-            def fourth():
-                @only("inner")
-                def _():
-                    one[1][k].wait_recv()
-                    two.wait_recv()
-                    low.wait_recv()
-
-                    def add(at):
-                        hs[g, k, 0, at, :] = (total(at) + zr[g, k, at, :].astype(F32)).astype(BF16)
-
-                    tiled(part, step, add)
-                    send(mids[0], "inner")
-
-            def fifth():
-                @only("inner")
-                def _():
-                    for n in range(len(mids)):
-                        mids[n].wait_recv()
-
-                        def add(at):
-                            value = (hs[g, k, n, at, :].astype(F32) + hr[g, k, n, at, :].astype(F32)).astype(BF16)
-                            if n + 1 == len(mids):
-                                got[g, bit["y"], k, at, :] = value
-                            else:
-                                hs[g, k, n + 1, at, :] = value
-
-                        tiled(part, step, add)
-                        if n + 1 < len(mids):
-                            send(mids[n + 1], "inner")
-                    send(up, "inner")
-                    send(last, "inner")
-
-            def ends():
-                @only("outer")
-                def _():
-                    up.wait_recv()
-                    send(last, "outer")
-
-            for name, task in dict(C2=second, C3=third_step, C4=fourth, C5=fifth, E5=ends).items():
-                tasks[f"{name}{g}{k}"] = task
-
-        for k in range(2):
-            half_tasks(k)
+                    if n + 1 < len(mids):
+                        send(mids[n + 1], "inner")
+                send(up, "inner")
+                send(last, "inner")
+
+        def ends():
+            @only("outer")
+            def _():
+                up.wait_recv()
+                send(last, "outer")
+
+            finish_part(bit["y"])
+
+        def finish_part(y):
+            local(got.at[b, y], grads.at[CUTS * y + k, :, pl.ds(g * wide, wide)], part_sem.at[0]).start()
 
         def seventh():
-            for copy in arrivals:
-                copy.wait_recv()
-            for a in range(2):
-                for k in range(2):
-                    out = grads.at[2 * a + k, :, pl.ds(g * wide, wide)]
-                    put(local(got.at[g, a, k], out, out_sem.at[g, 2 * a + k]))
-
-        tasks[f"C7{g}"] = seventh
+            last.wait_recv()
+            finish_part(1 - bit["y"])
+
+        names = dict(T=theirs, O=ours, C2=second, C3=third_step, C4=fourth, C5=fifth, E5=ends, C7=seventh)
+        for name, task in names.items():
+            tasks[f"{name}.{b}"] = task
 
     written = []
 
@@ -424,8 +411,8 @@
         copy.start()
         written.append(copy)
 
-    for g in range(groups):
-        group_tasks(g)
+    for b in range(blocks):
+        block_tasks(b)
 
     def forward(index, first):
         base = pl.multiple_of(index * rows, 128)
@@ -484,19 +471,19 @@
         def finish():
             def run(i, carry):
                 at = pl.ds(pl.multiple_of(n * third + i * 16, 16), 16)
-                kout[at, :] = kacc[at, :].astype(BF16)
                 value = x[at, :].astype(F32)
                 inv = invs[at, :]
                 scaled = dn[at, :] * flat[...]
                 inner = jnp.mean(scaled * value, axis=1, keepdims=True)
-                x[at, :] = (inv * scaled - value * (inv * inv * inv * inner)).astype(BF16)
+                tg[at, :] = (inv * scaled - value * (inv * inv * inv * inner)).astype(BF16)
                 return carry
 
             lax.fori_loop(0, third // 16, run, 0, unroll=2)
             at = pl.ds(n * third, third)
-            put(local(x.at[at], token_grad.at[at], out_sem.at[groups, n]))
+            put(local(tg.at[at], token_grad.at[at], out_sem.at[n]))
             if n == 2:
-                put(local(kout, keys, out_sem.at[groups, 3]))
+                kout[...] = kacc[...].astype(BF16)
+                put(local(kout, keys, out_sem.at[3]))
 
         tasks[f"F{n}"] = finish
 
@@ -506,26 +493,45 @@
     assert sorted(ORDER) == sorted(tasks)
     for name in ORDER:
         tasks[name]()
+
+    def left(kind, ref):
+        local(ref, ref, send_sem.at[KINDS.index(kind)]).wait()
+
+    def left_units(count):
+        if count >= 8:
+            left("far", full.at[pl.ds(0, count // 8)])
+        if count % 8:
+            left("far", full.at[0, pl.ds(0, count % 8 * unit)])
+
+    half = got.at[pl.ds(0, blocks // 2)]
+    for kind, ref in (("core", th), ("one", s1), ("two", s2), ("last", half)):
+        left(kind, ref)
+    left_units(sent[None])
+
+    @only("inner")
+    def _():
+        left("mid", hs)
+        left("up", half)
+        left_units(sent["inner"])
+
+    @only("outer")
+    def _():
+        left("low", hs.at[:, 0])
+        left_units(sent["outer"])
+
+    local(got, got, part_sem.at[0]).wait()
     for copy in written:
         copy.wait()
-    for role, copy in sent:
-        if role is None:
-            copy.wait_send()
-    for role in ("inner", "outer"):
-        @only(role)
-        def _():
-            for where, copy in sent:
-                if where == role:
-                    copy.wait_send()
 
 
 def layer(counts, tokens, gain, key_grad, weight):
     count, features = tokens.shape
     width = key_grad.shape[1]
     rows = weight.shape[0]
-    groups = len(HALVES)
-    wide = width // groups
-    part = rows // 4
+    blocks = len(HALVES)
+    assert blocks == GROUPS * CUTS
+    wide = width // GROUPS
+    part = rows // (2 * CUTS)
     hops = 1 + bits_of(counts["rep"]) - 3
     lanes = 128
     any_space = pl.BlockSpec(memory_space=pl.ANY)
@@ -538,37 +544,39 @@
         pltpu.VMEM((count, features), BF16),
         pltpu.VMEM((features, count), BF16),
         pltpu.VMEM((4, rows, width), BF16),
-        pltpu.VMEM((groups, 2, 2, part, wide), F32),
-        pltpu.VMEM((groups, 2, 4, part, wide), BF16),
-        pltpu.VMEM((groups, 2, 4, part, wide), BF16),
-        pltpu.VMEM((groups, 2, 2, part, wide), BF16),
-        pltpu.VMEM((groups, 2, 2, part, wide), BF16),
-        pltpu.VMEM((groups, 2, part, wide), BF16),
-        pltpu.VMEM((groups, 2, part, wide), BF16),
-        pltpu.VMEM((groups, 2, part, wide), BF16),
-        pltpu.VMEM((groups, 2, part, wide), BF16),
-        pltpu.VMEM((groups, 2, hops, part, wide), BF16),
-        pltpu.VMEM((groups, 2, hops, part, wide), BF16),
-        pltpu.VMEM((groups, 2, 2, part, wide), BF16),
+        pltpu.VMEM((blocks, 2, part, wide), F32),
+        pltpu.VMEM((blocks, 2, 2, part, wide), BF16),
+        pltpu.VMEM((blocks, 2, 2, part, wide), BF16),
+        pltpu.VMEM((blocks, 2, part, wide), BF16),
+        pltpu.VMEM((blocks, 2, part, wide), BF16),
+        pltpu.VMEM((blocks, part, wide), BF16),
+        pltpu.VMEM((blocks, part, wide), BF16),
+        pltpu.VMEM((blocks, part, wide), BF16),
+        pltpu.VMEM((blocks, hops, part, wide), BF16),
+        pltpu.VMEM((blocks, hops, part, wide), BF16),
+        pltpu.VMEM((blocks, 2, part, wide), BF16),
         pltpu.VMEM((count, width), F32),
         pltpu.VMEM((count, features), F32),
+        pltpu.VMEM((count, features), BF16),
         pltpu.VMEM((count, width), BF16),
         pltpu.VMEM((count, 1), F32),
         pltpu.VMEM((1, features), F32),
         dma((6,)),
-        dma((groups + 1, 4)),
-        dma((groups, 2)),
-        dma((groups, 2, 2, 2)),
-        dma((groups, 2, 2)),
-        dma((groups, 2, 2)),
-        dma((groups, 2, hops, 2)),
-        dma((groups, 2, 2)),
-        dma((groups, 2, 2)),
+        dma((4,)),
+        dma((1,)),
+        dma((len(KINDS),)),
+        dma((blocks,)),
+        dma((blocks, 2)),
+        dma((blocks,)),
+        dma((blocks,)),
+        dma((blocks, hops)),
+        dma((blocks,)),
+        dma((blocks,)),
+        dma((spreads,)),
+        dma((spreads, 3)),
         dma((spreads, 2)),
-        dma((spreads, 3, 2)),
-        dma((spreads, 2, 2)),
-        dma((spreads, 4, 2)),
-        dma((2,)),
+        dma((spreads, 4)),
+        dma((1,)),
     ]
     keys, token_grad, grads = pl.pallas_call(
         functools.partial(layer_kernel, counts),
@@ -577,7 +585,7 @@
         out_shape=[
             jax.ShapeDtypeStruct((count, width), BF16),
             jax.ShapeDtypeStruct((count, features), BF16),
-            jax.ShapeDtypeStruct((4, part, width), BF16),
+            jax.ShapeDtypeStruct((2 * CUTS, part, width), BF16),
         ],
         scratch_shapes=scratch,
         compiler_params=pltpu.CompilerParams(

time: 99.1 us -> 96 us (0.969)
  Pallas kernels: 98.2 us -> 95.1 us
    pallas_call x1, Pallas kernels: 88.2 us -> 85.1 us  [layer(): pl.pallas_call(functools.partial(layer_kernel, counts), in_specs=[any_spa...]
where the time goes in v2:
time: 96 us; the launch traced here: 95.9 us
  Pallas kernels  95.1 us (99%)
    pallas_call x1, Pallas kernels, layer(): pl.pallas_call(functools.partial(layer_kernel, counts), in_specs=[any_spa...  85.1 us
    pallas_call x1, Pallas kernels, requantize(): pl.pallas_call(functools.partial(requantize_kernel, chunks, sub), grid=(r...  10 us

profile of v2, /device:TPU:0, one launch (start us, length us, event | category | flops | bytes accessed | tf_op | source)
XLA Modules:
  0.0 95.9 jit_solution(2366269123648218320)
XLA Ops:
  0.6 85.1 %layer.1 = (bf16[384,1024]{1,0:T(8,128)(2,1)}, bf16[384,4608]{1,0:T(8,128)(2,1)}, bf16[6,192,1024]{2,1,0:T(8,128)(2,1)}) custom-call(bf16[384,4608]{1,0:T(8,128)(2,1)} %tokens.1, f32[36,128]{1,0:T(8,128)} %bitcast.7, bf16[384,1024]{1,0:T(8,128)(2,1)} %key_grad.1, bf16[1152,1024]{1,0:T(8,128)(2,1)} %weight.1), custom_call_target="tpu_custom_call" | custom-call | tf_op jit(solution)/shard_map/layer/pallas_call | solution.py:581
  85.7 10.0 %requantize.1 = (f32[1152,1024]{1,0:T(8,128)}, bf16[1152,1024]{1,0:T(8,128)(2,1)}, f32[4,1152]{1,0:T(4,128)}, bf16[1152,1024]{1,0:T(8,128)(2,1)}, f32[4,1152]{1,...) custom-call(bf16[1152,1024]{1,0:T(8,128)(2,1)} %bitcast.6, bf16[1152,1024]{1,0:T(8,128)(2,1)} %m_code.1, ...), custom_call_target="tpu_custom_call" | custom-call | tf_op jit(solution)/shard_map/requantize/pallas_call | solution.py:662

commit v3 on v2

--- a/solution.py
+++ b/solution.py
@@ -15,20 +15,21 @@
 GROUPS = 4
 CUTS = 3
 HALVES = [
-    "x", "y", "x", "x", "y", "y", "y", "x", "y", "y", "y", "y",
+    "x", "x", "y", "z", "y", "x", "y", "y", "y", "y", "y", "y",
 ]
 KINDS = ["core", "one", "two", "low", "mid", "up", "last", "far"]
-SPREADS = [2, 2, 4]
+SPREADS = [2, 4, 2]
 ORDER = [
-    "N0", "N1", "N2", "RT", "GATE", "WX0", "T.8", "T.6", "RO", "T.9", "WX2", "O.8", "T.4", "T.10", "O.9", "T.1",
-    "T.3", "WF0", "T.11", "T.5", "O.11", "WX1", "O.6", "T.7", "T.2", "WF2", "C2.9", "WC", "C2.8", "T.0", "O.1",
-    "WF1", "O.4", "C2.1", "O.3", "QB2", "O.7", "QA2", "BO", "C3.8", "C3.9", "O.5", "C2.3", "C4.8", "C2.5", "KO",
-    "QC2", "C3.1", "O.2", "C2.7", "C3.3", "O.10", "C3.5", "WG0", "C5.8", "C4.1", "KC", "C2.4", "C2.2", "C2.11",
-    "C3.7", "C4.9", "C4.5", "E5.8", "C2.10", "C5.1", "C4.7", "C5.9", "O.0", "QD2", "WG1", "C3.4", "QE2", "E5.1",
-    "C3.2", "C5.5", "E5.9", "C4.3", "C3.11", "BC", "C5.7", "E5.5", "C7.8", "C4.4", "C4.2", "C3.10", "C2.6",
-    "C5.4", "C4.11", "C2.0", "C5.3", "C7.1", "E5.7", "C7.9", "KG", "C4.10", "KF", "C3.0", "C5.11", "E5.4", "BF",
-    "E5.3", "C3.6", "C5.2", "C7.4", "E5.11", "C4.0", "C7.7", "C5.10", "C7.5", "BG", "E5.2", "C4.6", "F0",
-    "C7.3", "E5.10", "C5.0", "F1", "C7.11", "C5.6", "F2", "E5.0", "C7.2", "C7.10", "E5.6", "C7.0", "C7.6",
+    "N0", "N1", "N2", "GATE", "WX1", "RT", "T.11", "T.7", "T.10", "RO", "WX2", "O.11", "WX0", "O.7", "WF1",
+    "T.4", "T.2", "T.0", "T.3", "T.8", "O.4", "C2.11", "C2.7", "O.10", "T.9", "O.0", "WF2", "T.1", "WC", "O.8",
+    "T.5", "QA1", "O.2", "QB1", "C3.11", "C3.7", "T.6", "WF0", "C2.0", "C2.8", "C4.7", "O.9", "O.5", "QC1",
+    "C4.11", "KO", "C2.10", "C5.7", "KC", "C2.5", "C3.8", "C5.11", "QD1", "BC", "C2.2", "C3.0", "C3.10", "C2.9",
+    "C2.4", "O.3", "C3.5", "C4.8", "WG0", "C4.0", "C4.10", "WG2", "O.6", "C3.9", "BO", "C5.0", "C3.2", "C5.8",
+    "C4.5", "C4.9", "C5.10", "E5.7", "QE1", "C2.6", "C3.4", "E5.11", "O.1", "KF", "D2.3", "C4.2", "C5.5",
+    "E5.0", "KG", "D3.3", "E5.8", "C7.7", "C7.11", "BG", "C7.0", "C2.1", "C5.2", "D4.3", "C3.6", "E5.10",
+    "C4.4", "BF", "C4.6", "E5.2", "C3.1", "D5.3", "C7.8", "C5.9", "F0", "C5.4", "F1", "E5.5", "C4.1", "F2",
+    "C5.6", "C7.2", "C5.1", "C7.10", "D6.3", "E5.9", "E5.4", "E5.6", "D7.3", "C7.9", "E5.1", "C7.5", "C7.4",
+    "C7.6", "D8.3", "C7.1",
 ]
 
 
@@ -49,6 +50,7 @@
             self.of[f"h{n}"] = ("rep", n)
         self.bit = {label: self.digit(axis, 1 << n, 2) for label, (axis, n) in self.of.items()}
         self.place = self.digit("rep", 2, 4)
+        self.side = lax.div(self.place, jnp.int32(2))
         self.inner = lax.rem(lax.div(self.place + 1, jnp.int32(2)), jnp.int32(2)) == 1
 
     def digit(self, axis, unit, base):
@@ -77,7 +79,7 @@
 
 
 def layer_kernel(counts, tokens, gain, key_grad, weight, keys, token_grad, grads, *scratch):
-    (x, gains, kg, normed, turned, full, own, th, kc, s1, r1, s2, r2, zr, hs, hr, got, kacc, dn, tg, kout, invs, flat,
+    (x, gains, kg, normed, turned, full, own, th, kc, s1, r1, s2, r2, zr, hs, hr, got, kacc, dn, tg, invs, flat,
      load_sem, out_sem, part_sem, send_sem, core_sem, one_sem, two_sem, low_sem, mid_sem, up_sem, a_sem, wx_sem, wl_sem, wm_sem, wc_sem,
      wo_sem) = scratch
     lab = Labels(counts)
@@ -294,11 +296,104 @@
 
     step = step_of(part, 96)
 
+    def late_tasks(b, one, out_at, finish_part):
+        e = blocks + HALVES[:b].count("z")
+        second = lab.side
+        spots = (1 - second, second)
+        stores = (b, e)
+        lanes = ["y", *lab.extra]
+        lows = [remote(hs.at[s, 0], zr.at[s], low_sem.at[s], "l", "low") for s in stores]
+        over = remote(hs.at[b, 0], hr.at[b, 0], mid_sem.at[b, 0], "m", "mid")
+        chain = [remote(hs.at[e, n], hr.at[e, n], mid_sem.at[e, n], label, "mid") for n, label in enumerate(lanes)]
+        mine, other = got.at[b, second], got.at[b, 1 - second]
+        back = remote(mine, mine, a_sem.at[b], "m", "mid")
+        ups = [remote(mine, out_at(second), up_sem.at[b], "l", "up"), remote(other, out_at(1 - second), up_sem.at[e], "l", "up")]
+
+        def total(n, at):
+            return own[b, spots[n], at, :] + r1[b, spots[n], at, :].astype(F32)
+
+        def down(n):
+            @only("outer")
+            def _():
+                one[n].wait_recv()
+
+                def add(at):
+                    hs[stores[n], 0, at, :] = total(n, at).astype(BF16)
+
+                tiled(part, step, add)
+                send(lows[n], "outer")
+
+        def fourth():
+            @only("inner")
+            def _():
+                one[0].wait_recv()
+                lows[0].wait_recv()
+
+                def add(at):
+                    hs[b, 0, at, :] = (total(0, at) + zr[b, at, :].astype(F32)).astype(BF16)
+
+                tiled(part, step, add)
+                send(over, "inner")
+
+        def fifth():
+            @only("inner")
+            def _():
+                one[1].wait_recv()
+                lows[1].wait_recv()
+                over.wait_recv()
+
+                def add(at):
+                    value = total(1, at) + zr[e, at, :].astype(F32)
+                    hs[e, 0, at, :] = (value + hr[b, 0, at, :].astype(F32)).astype(BF16)
+
+                tiled(part, step, add)
+                send(chain[0], "inner")
+
+        def sixth():
+            @only("inner")
+            def _():
+                for n in range(len(chain)):
+                    chain[n].wait_recv()
+
+                    def add(at):
+                        value = (hs[e, n, at, :].astype(F32) + hr[e, n, at, :].astype(F32)).astype(BF16)
+                        if n + 1 == len(chain):
+                            got[b, second, at, :] = value
+                        else:
+                            hs[e, n + 1, at, :] = value
+
+                    tiled(part, step, add)
+                    if n + 1 < len(chain):
+                        send(chain[n + 1], "inner")
+                send(back, "inner")
+                send(ups[0], "inner")
+                finish_part(second)
+
+        def seventh():
+            @only("inner")
+            def _():
+                back.wait_recv()
+                send(ups[1], "inner")
+                finish_part(1 - second)
+
+        def eighth():
+            @only("outer")
+            def _():
+                for copy in ups:
+                    copy.wait_recv()
+
+        return dict(D2=lambda: down(0), D3=lambda: down(1), D4=fourth, D5=fifth, D6=sixth, D7=seventh, D8=eighth)
+
     def block_tasks(b):
-        o1 = HALVES[b]
-        o2 = "y" if o1 == "x" else "x"
-        b1, b2 = bit[o1], bit[o2]
+        late = HALVES[b] == "z"
+        o1 = "y" if HALVES[b] == "y" else "x"
+        o2 = "x" if o1 == "y" else "y"
+        b1 = bit[o1]
+        b2 = lab.side if late else bit[o2]
         g, k = b // CUTS, b % CUTS
+        def out_at(y):
+            return grads.at[CUTS * y + k, :, pl.ds(g * wide, wide)]
+
         over = remote(th.at[b], kc.at[b], core_sem.at[b], "c", "core")
         one = [remote(s1.at[b, j], r1.at[b, j], one_sem.at[b, n], o1, "one") for n, j in enumerate((1 - b2, b2))]
         two = remote(s2.at[b], r2.at[b], two_sem.at[b], o2, "two")
@@ -307,7 +402,7 @@
         mids = [remote(hs.at[b, n], hr.at[b, n], mid_sem.at[b, n], label, "mid") for n, label in enumerate(lanes)]
         mine = got.at[b, bit["y"]]
         up = remote(mine, mine, up_sem.at[b], "l", "up")
-        last = remote(mine, mine, a_sem.at[b], "y", "last")
+        last = remote(mine, out_at(bit["y"]), a_sem.at[b], "y", "last")
 
         def theirs():
             once(load_kg)
@@ -395,13 +490,15 @@
             finish_part(bit["y"])
 
         def finish_part(y):
-            local(got.at[b, y], grads.at[CUTS * y + k, :, pl.ds(g * wide, wide)], part_sem.at[0]).start()
+            local(got.at[b, y], out_at(y), part_sem.at[0]).start()
 
         def seventh():
             last.wait_recv()
-            finish_part(1 - bit["y"])
-
-        names = dict(T=theirs, O=ours, C2=second, C3=third_step, C4=fourth, C5=fifth, E5=ends, C7=seventh)
+
+        if late:
+            names = dict(T=theirs, O=ours, **late_tasks(b, one, out_at, finish_part))
+        else:
+            names = dict(T=theirs, O=ours, C2=second, C3=third_step, C4=fourth, C5=fifth, E5=ends, C7=seventh)
         for name, task in names.items():
             tasks[f"{name}.{b}"] = task
 
@@ -482,8 +579,9 @@
             at = pl.ds(n * third, third)
             put(local(tg.at[at], token_grad.at[at], out_sem.at[n]))
             if n == 2:
-                kout[...] = kacc[...].astype(BF16)
-                put(local(kout, keys, out_sem.at[3]))
+                assert all(ORDER.index(f"O.{b}") < ORDER.index("F2") for b in range(blocks))
+                kg[...] = kacc[...].astype(BF16)
+                put(local(kg, keys, out_sem.at[3]))
 
         tasks[f"F{n}"] = finish
 
@@ -503,23 +601,38 @@
         if count % 8:
             left("far", full.at[0, pl.ds(0, count % 8 * unit)])
 
-    half = got.at[pl.ds(0, blocks // 2)]
-    for kind, ref in (("core", th), ("one", s1), ("two", s2), ("last", half)):
-        left(kind, ref)
+    def left_pieces(sem, count):
+        while count > 0:
+            take = min(count, 2 * blocks)
+            for ref in ([s1.at[pl.ds(0, take // 2)]] if take > 1 else []) + ([s1.at[0, 0]] if take % 2 else []):
+                local(ref, ref, sem).wait()
+            count -= take
+
+    def left_kind(kind, count):
+        left_pieces(send_sem.at[KINDS.index(kind)], count)
+
+    twice = HALVES.count("z")
+    once_only = blocks - twice
+    hops = hs.shape[1]
+    left("core", th)
+    left("one", s1)
+    left_kind("two", once_only)
+    left_kind("last", once_only)
     left_units(sent[None])
 
     @only("inner")
     def _():
-        left("mid", hs)
-        left("up", half)
+        left_kind("mid", once_only * hops + twice * (2 + hops))
+        left_kind("up", once_only + 2 * twice)
+        left_pieces(part_sem.at[0], once_only + 2 * twice)
         left_units(sent["inner"])
 
     @only("outer")
     def _():
-        left("low", hs.at[:, 0])
+        left_kind("low", once_only + 2 * twice)
+        left_pieces(part_sem.at[0], once_only)
         left_units(sent["outer"])
 
-    local(got, got, part_sem.at[0]).wait()
     for copy in written:
         copy.wait()
 
@@ -534,6 +647,7 @@
     part = rows // (2 * CUTS)
     hops = 1 + bits_of(counts["rep"]) - 3
     lanes = 128
+    stores = blocks + HALVES.count("z")
     any_space = pl.BlockSpec(memory_space=pl.ANY)
     dma = pltpu.SemaphoreType.DMA
     spreads = len(SPREADS)
@@ -551,14 +665,13 @@
         pltpu.VMEM((blocks, 2, part, wide), BF16),
         pltpu.VMEM((blocks, part, wide), BF16),
         pltpu.VMEM((blocks, part, wide), BF16),
-        pltpu.VMEM((blocks, part, wide), BF16),
-        pltpu.VMEM((blocks, hops, part, wide), BF16),
-        pltpu.VMEM((blocks, hops, part, wide), BF16),
+        pltpu.VMEM((stores, part, wide), BF16),
+        pltpu.VMEM((stores, hops, part, wide), BF16),
+        pltpu.VMEM((stores, hops, part, wide), BF16),
         pltpu.VMEM((blocks, 2, part, wide), BF16),
         pltpu.VMEM((count, width), F32),
         pltpu.VMEM((count, features), F32),
         pltpu.VMEM((count, features), BF16),
-        pltpu.VMEM((count, width), BF16),
         pltpu.VMEM((count, 1), F32),
         pltpu.VMEM((1, features), F32),
         dma((6,)),
@@ -568,9 +681,9 @@
         dma((blocks,)),
         dma((blocks, 2)),
         dma((blocks,)),
-        dma((blocks,)),
-        dma((blocks, hops)),
-        dma((blocks,)),
+        dma((stores,)),
+        dma((stores, hops)),
+        dma((stores,)),
         dma((blocks,)),
         dma((spreads,)),
         dma((spreads, 3)),

time: 96 us -> 94.2 us (0.981)
  Pallas kernels: 95.1 us -> 93.2 us
    pallas_call x1, Pallas kernels: 85.1 us -> 83.2 us  [layer(): pl.pallas_call(functools.partial(layer_kernel, counts), in_specs=[any_spa...]
where the time goes in v3:
time: 94.2 us; the launch traced here: 94 us
  Pallas kernels  93.2 us (99%)
    pallas_call x1, Pallas kernels, layer(): pl.pallas_call(functools.partial(layer_kernel, counts), in_specs=[any_spa...  83.2 us
    pallas_call x1, Pallas kernels, requantize(): pl.pallas_call(functools.partial(requantize_kernel, chunks, sub), grid=(r...  10 us

profile of v3, /device:TPU:0, one launch (start us, length us, event | category | flops | bytes accessed | tf_op | source)
XLA Modules:
  0.0 94.0 jit_solution(9848744900680625580)
XLA Ops:
  0.6 83.2 %layer.1 = (bf16[384,1024]{1,0:T(8,128)(2,1)}, bf16[384,4608]{1,0:T(8,128)(2,1)}, bf16[6,192,1024]{2,1,0:T(8,128)(2,1)}) custom-call(bf16[384,4608]{1,0:T(8,128)(2,1)} %tokens.1, f32[36,128]{1,0:T(8,128)} %bitcast.7, bf16[384,1024]{1,0:T(8,128)(2,1)} %key_grad.1, bf16[1152,1024]{1,0:T(8,128)(2,1)} %weight.1), custom_call_target="tpu_custom_call" | custom-call | tf_op jit(solution)/shard_map/layer/pallas_call | solution.py:694
  83.8 10.0 %requantize.1 = (f32[1152,1024]{1,0:T(8,128)}, bf16[1152,1024]{1,0:T(8,128)(2,1)}, f32[4,1152]{1,0:T(4,128)}, bf16[1152,1024]{1,0:T(8,128)(2,1)}, f32[4,1152]{1,...) custom-call(bf16[1152,1024]{1,0:T(8,128)(2,1)} %bitcast.6, bf16[1152,1024]{1,0:T(8,128)(2,1)} %m_code.1, ...), custom_call_target="tpu_custom_call" | custom-call | tf_op jit(solution)/shard_map/requantize/pallas_call | solution.py:775

commit v4 on v3

--- a/solution.py
+++ b/solution.py
@@ -119,10 +119,11 @@
         return pl.when(inner if role == "inner" else jnp.logical_not(inner))
 
     third = tokens_here // 3
-    loads = [local(tokens.at[pl.ds(n * third, third)], x.at[pl.ds(n * third, third)], load_sem.at[n]) for n in range(3)]
-    load_gain = local(gain, gains, load_sem.at[3])
-    load_kg = local(key_grad, kg, load_sem.at[4])
-    load_w = local(weight, full.at[shard], load_sem.at[5])
+    sixth = tokens_here // 6
+    loads = [local(tokens.at[pl.ds(n * sixth, sixth)], x.at[pl.ds(n * sixth, sixth)], load_sem.at[n]) for n in range(6)]
+    load_gain = local(gain, gains, load_sem.at[6])
+    load_kg = local(key_grad, kg, load_sem.at[7])
+    load_w = local(weight, full.at[shard], load_sem.at[8])
     load_gain.start()
     for load in loads:
         load.start()
@@ -255,33 +256,45 @@
             if n == 0:
                 load_gain.wait()
                 flat[...] = jnp.concatenate([gains[k : k + 1, :] for k in range(features // gains.shape[1])], axis=1)
-            loads[n].wait()
-
-            def run(i, carry):
-                at = pl.ds(pl.multiple_of(n * third + i * 16, 16), 16)
-                value = x[at, :].astype(F32)
-                inv = lax.rsqrt(jnp.mean(value * value, axis=1, keepdims=True) + 1e-06)
-                invs[at, :] = inv
-                normed[at, :] = (value * inv * flat[...]).astype(BF16)
-                return carry
-
-            lax.fori_loop(0, third // 16, run, 0, unroll=4)
+            for half in range(2):
+                loads[2 * n + half].wait()
+                if n:
+                    turn(1 - core, n - 1, half)
+                for i in range(sixth // 16):
+                    at = pl.ds(n * third + half * sixth + i * 16, 16)
+                    value = x[at, :].astype(F32)
+                    inv = lax.rsqrt(jnp.mean(value * value, axis=1, keepdims=True) + 1e-06)
+                    invs[at, :] = inv
+                    normed[at, :] = (value * inv * flat[...]).astype(BF16)
 
         tasks[f"N{n}"] = norm
 
+    def turn(half, n, a):
+        here = slice(n * third, (n + 1) * third)
+        for i in range(rows // 128):
+            at = pl.ds(pl.multiple_of((2 * a + half) * rows + i * 128, 128), 128)
+            turned[at, here] = normed[here, at].T
+
     def turn_task(name, half):
-        def turn():
-            for a in range(2):
-                base = (2 * a + half) * rows
-
-                def run(i, carry):
-                    at = pl.ds(pl.multiple_of(base + i * 128, 128), 128)
-                    turned[at, :] = normed[:, at].T
-                    return carry
-
-                lax.fori_loop(0, rows // 128, run, 0, unroll=3)
-
-        tasks[name] = turn
+        def task():
+            if half is core:
+                for a in range(2):
+                    base = (2 * a + half) * rows
+
+                    def run(i, carry):
+                        at = pl.ds(pl.multiple_of(base + i * 128, 128), 128)
+                        turned[at, :] = normed[:, at].T
+                        return carry
+
+                    lax.fori_loop(0, rows // 128, run, 0, unroll=3)
+            else:
+                for a in range(2):
+                    turn(half, 2, a)
+
+        tasks[name] = task
+
+    for n in range(3):
+        norm_task(n)
 
     turn_task("RT", 1 - core)
     turn_task("RO", core)
@@ -305,8 +318,8 @@
         lows = [remote(hs.at[s, 0], zr.at[s], low_sem.at[s], "l", "low") for s in stores]
         over = remote(hs.at[b, 0], hr.at[b, 0], mid_sem.at[b, 0], "m", "mid")
         chain = [remote(hs.at[e, n], hr.at[e, n], mid_sem.at[e, n], label, "mid") for n, label in enumerate(lanes)]
-        mine, other = got.at[b, second], got.at[b, 1 - second]
-        back = remote(mine, mine, a_sem.at[b], "m", "mid")
+        mine, other = got.at[b], got.at[e]
+        back = remote(mine, other, a_sem.at[b], "m", "mid")
         ups = [remote(mine, out_at(second), up_sem.at[b], "l", "up"), remote(other, out_at(1 - second), up_sem.at[e], "l", "up")]
 
         def total(n, at):
@@ -358,7 +371,7 @@
                     def add(at):
                         value = (hs[e, n, at, :].astype(F32) + hr[e, n, at, :].astype(F32)).astype(BF16)
                         if n + 1 == len(chain):
-                            got[b, second, at, :] = value
+                            got[b, at, :] = value
                         else:
                             hs[e, n + 1, at, :] = value
 
@@ -374,7 +387,7 @@
             def _():
                 back.wait_recv()
                 send(ups[1], "inner")
-                finish_part(1 - second)
+                finish_part(1 - second, e)
 
         def eighth():
             @only("outer")
@@ -400,7 +413,7 @@
         low = remote(hs.at[b, 0], zr.at[b], low_sem.at[b], "l", "low")
         lanes = ["m", *lab.extra]
         mids = [remote(hs.at[b, n], hr.at[b, n], mid_sem.at[b, n], label, "mid") for n, label in enumerate(lanes)]
-        mine = got.at[b, bit["y"]]
+        mine = got.at[b]
         up = remote(mine, mine, up_sem.at[b], "l", "up")
         last = remote(mine, out_at(bit["y"]), a_sem.at[b], "y", "last")
 
@@ -471,7 +484,7 @@
                     def add(at):
                         value = (hs[b, n, at, :].astype(F32) + hr[b, n, at, :].astype(F32)).astype(BF16)
                         if n + 1 == len(mids):
-                            got[b, bit["y"], at, :] = value
+                            got[b, at, :] = value
                         else:
                             hs[b, n + 1, at, :] = value
 
@@ -489,8 +502,8 @@
 
             finish_part(bit["y"])
 
-        def finish_part(y):
-            local(got.at[b, y], out_at(y), part_sem.at[0]).start()
+        def finish_part(y, spot=b):
+            local(got.at[spot], out_at(y), part_sem.at[0]).start()
 
         def seventh():
             last.wait_recv()
@@ -668,13 +681,13 @@
         pltpu.VMEM((stores, part, wide), BF16),
         pltpu.VMEM((stores, hops, part, wide), BF16),
         pltpu.VMEM((stores, hops, part, wide), BF16),
-        pltpu.VMEM((blocks, 2, part, wide), BF16),
+        pltpu.VMEM((stores, part, wide), BF16),
         pltpu.VMEM((count, width), F32),
         pltpu.VMEM((count, features), F32),
         pltpu.VMEM((count, features), BF16),
         pltpu.VMEM((count, 1), F32),
         pltpu.VMEM((1, features), F32),
-        dma((6,)),
+        dma((9,)),
         dma((4,)),
         dma((1,)),
         dma((len(KINDS),)),
@@ -709,22 +722,39 @@
     return keys, token_grad, grads.reshape(rows, width)
 
 
-def requantize_kernel(
-    chunks, sub, grads, m_code, m_exp, v_code, v_exp, keys_in, token_in,
-    step, m_rel, m_scale, v_rel, v_scale, keys_out, token_out,
-    units, tops, keys, token, sems,
-):
-    here, last = pl.program_id(0), pl.num_programs(0) - 1
-    into = [pltpu.make_async_copy(token_in, token, sems.at[0]), pltpu.make_async_copy(keys_in, keys, sems.at[1])]
-    back = [pltpu.make_async_copy(token, token_out, sems.at[2]), pltpu.make_async_copy(keys, keys_out, sems.at[3])]
-
-    @pl.when(here == 0)
-    def _():
-        for copy in into:
-            copy.start()
-
+def requantize_kernel(chunks, block, ahead, *refs):
+    ins, outs = refs[:5], refs[7:12]
+    pass_in, pass_out = refs[5:7], refs[12:14]
+    grads, m_code, v_code, m_exp, v_exp, step, m_rel, v_rel, m_scale, v_scale, units = refs[14:25]
+    passed = refs[25:27]
+    in_sem, exp_sem, out_sem, scale_sem, pass_sem = refs[27:]
     rows, width = m_code.shape
     size = width // chunks
+    count = rows // block
+
+    def at_block(i):
+        return pl.ds(pl.multiple_of(i * block, block), block)
+
+    def load(i, n):
+        return pltpu.make_async_copy(ins[n].at[at_block(i)], (grads, m_code, v_code)[n].at[at_block(i)], in_sem.at[i, n])
+
+    def store(i, n):
+        return pltpu.make_async_copy((step, m_rel, v_rel)[n].at[at_block(i)], outs[n].at[at_block(i)], out_sem.at[i, n])
+
+    exps = [pltpu.make_async_copy(ins[3 + n], (m_exp, v_exp)[n], exp_sem.at[n]) for n in range(2)]
+    scales = [pltpu.make_async_copy((m_scale, v_scale)[n], outs[3 + n], scale_sem.at[n]) for n in range(2)]
+    into = [pltpu.make_async_copy(pass_in[n], passed[n], pass_sem.at[n]) for n in range(2)]
+    back = [pltpu.make_async_copy(passed[n], pass_out[n], pass_sem.at[2 + n]) for n in range(2)]
+
+    for copy in exps:
+        copy.start()
+    for i in range(ahead):
+        for n in range(3):
+            load(i, n).start()
+    for copy in into:
+        copy.start()
+    for copy in exps:
+        copy.wait()
     unit_m = jnp.exp2(m_exp[...].astype(F32)) * (0.9 / 127.0)
     unit_v = jnp.exp2(v_exp[...].astype(F32)) * (0.999 / 255.0)
     units[...] = jnp.concatenate([unit_m, unit_v], axis=0).T
@@ -732,7 +762,15 @@
     rate = bias_second**0.5 / bias_first
 
     def run(i, carry):
-        at = pl.ds(pl.multiple_of(i * sub, sub), sub)
+        @pl.when(i + ahead < count)
+        def _():
+            for n in range(3):
+                load(i + ahead, n).start()
+
+        for n in range(3):
+            load(i, n).wait()
+        at = at_block(i)
+        tops = [], []
         for c in range(chunks):
             cols = slice(c * size, (c + 1) * size)
             g = grads[at, cols].astype(F32)
@@ -742,59 +780,80 @@
             step[at, cols] = (m_new * rate) / (root + floor)
             m_top = jnp.max(jnp.abs(m_new), axis=1, keepdims=True)
             v_top = jnp.max(v_new, axis=1, keepdims=True)
-            tops[at, c : c + 1] = m_top
-            tops[at, chunks + c : chunks + c + 1] = v_top
+            tops[0].append(m_top)
+            tops[1].append(v_top)
             m_rel[at, cols] = (m_new * (1.0 / (m_top + 1e-06))).astype(BF16)
             v_rel[at, cols] = (v_new * (1.0 / (v_top + 1e-06))).astype(BF16)
+        turned = jnp.concatenate(tops[0] + tops[1], axis=1).T
+        m_scale[:, at] = turned[:chunks]
+        v_scale[:, at] = turned[chunks:]
+        for n in range(3):
+            store(i, n).start()
+
+        @pl.when(i == count // 2)
+        def _():
+            for one, other in zip(into, back):
+                one.wait()
+                other.start()
+
         return carry
 
-    lax.fori_loop(0, rows // sub, run, 0, unroll=True)
-    turned = tops[...].T
-    m_scale[...] = turned[:chunks]
-    v_scale[...] = turned[chunks:]
-
-    @pl.when(here == last - 1)
-    def _():
-        for one, other in zip(into, back):
-            one.wait()
-            other.start()
-
-    @pl.when(here == last)
-    def _():
-        for copy in back:
-            copy.wait()
-
-
-def requantize(grads, m_code, m_exp, v_code, v_exp, keys, token_grad, block=384, sub=128):
+    lax.fori_loop(0, count, run, 0)
+    for copy in scales:
+        copy.start()
+
+    def drain(i, carry):
+        for n in range(3):
+            store(i, n).wait()
+        return carry
+
+    lax.fori_loop(0, count, drain, 0)
+    for copy in back + scales:
+        copy.wait()
+
+
+def requantize(grads, m_code, m_exp, v_code, v_exp, keys, token_grad, block=128, ahead=4):
     rows, width = m_code.shape
     chunks = m_exp.shape[1]
-    wide = pl.BlockSpec((block, width), lambda i: (i, 0))
-    thin = pl.BlockSpec((chunks, block), lambda i: (0, i))
+    count = rows // block
     any_space = pl.BlockSpec(memory_space=pl.ANY)
     shape = jax.ShapeDtypeStruct
-    step, m_rel, m_scale, v_rel, v_scale, keys, token_grad = pl.pallas_call(
-        functools.partial(requantize_kernel, chunks, sub),
-        grid=(rows // block,),
-        in_specs=[wide, wide, thin, wide, thin, any_space, any_space],
-        out_specs=[wide, wide, thin, wide, thin, any_space, any_space],
+    dma = pltpu.SemaphoreType.DMA
+    step, m_rel, v_rel, m_scale, v_scale, keys, token_grad = pl.pallas_call(
+        functools.partial(requantize_kernel, chunks, block, min(ahead, count)),
+        in_specs=[any_space] * 7,
+        out_specs=[any_space] * 7,
         out_shape=[
             shape((rows, width), F32),
             shape((rows, width), BF16),
+            shape((rows, width), BF16),
             shape((chunks, rows), F32),
-            shape((rows, width), BF16),
             shape((chunks, rows), F32),
             shape(keys.shape, keys.dtype),
             shape(token_grad.shape, token_grad.dtype),
         ],
         scratch_shapes=[
-            pltpu.VMEM((block, 2 * chunks), F32),
-            pltpu.VMEM((block, 2 * chunks), F32),
+            pltpu.VMEM((rows, width), BF16),
+            pltpu.VMEM((rows, width), BF16),
+            pltpu.VMEM((rows, width), BF16),
+            pltpu.VMEM((chunks, rows), jnp.int32),
+            pltpu.VMEM((chunks, rows), jnp.int32),
+            pltpu.VMEM((rows, width), F32),
+            pltpu.VMEM((rows, width), BF16),
+            pltpu.VMEM((rows, width), BF16),
+            pltpu.VMEM((chunks, rows), F32),
+            pltpu.VMEM((chunks, rows), F32),
+            pltpu.VMEM((rows, 2 * chunks), F32),
             pltpu.VMEM(keys.shape, keys.dtype),
             pltpu.VMEM(token_grad.shape, token_grad.dtype),
-            pltpu.SemaphoreType.DMA((4,)),
+            dma((count, 3)),
+            dma((2,)),
+            dma((count, 3)),
+            dma((2,)),
+            dma((4,)),
         ],
         name="requantize",
-    )(grads, m_code, m_exp.T, v_code, v_exp.T, keys, token_grad)
+    )(grads, m_code, v_code, m_exp.T, v_exp.T, keys, token_grad)
     return keys, token_grad, step, m_rel, m_scale.T, v_rel, v_scale.T
 
 

time: 94.2 us -> 93.6 us (level)
  no operation moved by 1% of the time
where the time goes in v4:
time: 93.6 us; the launch traced here: 93.4 us
  Pallas kernels  92.6 us (99%)
    pallas_call x1, Pallas kernels, layer(): pl.pallas_call(functools.partial(layer_kernel, counts), in_specs=[any_spa...  83.1 us
    pallas_call x1, Pallas kernels, requantize(): pl.pallas_call(functools.partial(requantize_kernel, chunks, block, min(ah...  9.48 us

profile of v4, /device:TPU:0, one launch (start us, length us, event | category | flops | bytes accessed | tf_op | source)
XLA Modules:
  0.0 93.4 jit_solution(17774985694200738036)
XLA Ops:
  0.6 83.1 %layer.1 = (bf16[384,1024]{1,0:T(8,128)(2,1)}, bf16[384,4608]{1,0:T(8,128)(2,1)}, bf16[6,192,1024]{2,1,0:T(8,128)(2,1)}) custom-call(bf16[384,4608]{1,0:T(8,128)(2,1)} %tokens.1, f32[36,128]{1,0:T(8,128)} %bitcast.7, bf16[384,1024]{1,0:T(8,128)(2,1)} %key_grad.1, bf16[1152,1024]{1,0:T(8,128)(2,1)} %weight.1), custom_call_target="tpu_custom_call" | custom-call | tf_op jit(solution)/shard_map/layer/pallas_call | solution.py:707
  83.8 9.5 %requantize.1 = (f32[1152,1024]{1,0:T(8,128)}, bf16[1152,1024]{1,0:T(8,128)(2,1)}, bf16[1152,1024]{1,0:T(8,128)(2,1)}, f32[4,1152]{1,0:T(4,128)}, f32[4,1152]{1,...) custom-call(bf16[1152,1024]{1,0:T(8,128)(2,1)} %bitcast.6, bf16[1152,1024]{1,0:T(8,128)(2,1)} %refs_1_.1, ...), custom_call_target="tpu_custom_call" | custom-call | tf_op jit(solution)/shard_map/requantize/pallas_call | solution.py:822
